TPU v7x, 32 devices: a whole 2x2x4 slice. The times are simulated.
32 devices in a mesh: dp: 2 (over x), tpa: 4 (over z), tpb: 4 (over y, core).
Axes of the slice: x: 2, y: 2, z: 4, core: 2. Of those that a mesh axis runs over, the one named last changes fastest.
Arguments:
- hidden: bfloat16 [32, 25, 3072], P('dp'), parts along dimension 0
- w_head: bfloat16 [3072, 128256], P(None, ('tpa', 'tpb'))
- q_draft: float32 [32, 24, 128256], P(('dp', 'tpa', 'tpb')), parts along dimension 0
- x_draft: int32 [32, 24], P('dp'), parts along dimension 0
Outputs:
- output 1: float32 [32, 24], P('dp'), parts along dimension 0
- output 2: float32 [32], P('dp'), parts along dimension 0
- output 3: float32 [32, 24, 128256], P('dp', None, ('tpa', 'tpb')), parts along dimension 0
- output 4: float32 [32, 128256], P('dp', ('tpa', 'tpb')), parts along dimension 0
There are 2 independent parts. A program takes and returns all parts, laid end to end along the dimension named above; an argument that names none is the same for every part.
All inputs are finite; a program needn't handle non-finite values.
Results may differ from a plain program's by a relative error of at most 0.001.
Values are sent between devices in bfloat16 or wider.
A program may use at most 1 GiB of HBM per device.

v0:
```python
import jax
import jax.numpy as jnp
from jax import lax
from jax.sharding import PartitionSpec as P

INV_TEMP = 1.25
VOCAB_AXES = ("tpa", "tpb")


def solution(mesh):
    tpb_size = mesh.shape["tpb"]

    def local_step(hidden, w_head, q_draft, x_draft):
        num_draft = x_draft.shape[1]
        vocab_local = w_head.shape[1]
        logits = jnp.einsum("bgd,dv->bgv", hidden, w_head, preferred_element_type=jnp.float32) * INV_TEMP
        glob_max = lax.pmax(jnp.max(logits, axis=-1), VOCAB_AXES)
        exp_vals = jnp.exp(logits - glob_max[..., None])
        exp_sum = lax.psum(jnp.sum(exp_vals, axis=-1), VOCAB_AXES)
        prob_all = exp_vals / exp_sum[..., None]
        q_vocab = lax.all_to_all(q_draft, VOCAB_AXES, 2, 0, tiled=True)
        p_draft = prob_all[:, :num_draft, :]
        shard_idx = lax.axis_index("tpa") * tpb_size + lax.axis_index("tpb")
        local_ids = x_draft - shard_idx * vocab_local
        is_owned = (local_ids >= 0) & (local_ids < vocab_local)
        safe_ids = jnp.clip(local_ids, 0, vocab_local - 1)[..., None]
        p_pick = jnp.where(is_owned, jnp.take_along_axis(p_draft, safe_ids, axis=2)[..., 0], 0.0)
        q_pick = jnp.where(is_owned, jnp.take_along_axis(q_vocab, safe_ids, axis=2)[..., 0], 0.0)
        excess = jnp.maximum(p_draft - q_vocab, 0.0)
        reduced = lax.psum(jnp.stack([p_pick, q_pick, jnp.sum(excess, axis=-1)]), VOCAB_AXES)
        accept = jnp.minimum(1.0, reduced[0] / reduced[1])
        expected = jnp.sum(jnp.cumprod(accept, axis=1), axis=1)
        residual = excess / reduced[2][..., None]
        return accept, expected, residual, prob_all[:, num_draft, :]

    return jax.shard_map(
        local_step, mesh=mesh,
        in_specs=(P("dp", None, None), P(None, VOCAB_AXES), P(("dp",) + VOCAB_AXES, None, None), P("dp", None)),
        out_specs=(P("dp", None), P("dp"), P("dp", None, VOCAB_AXES), P("dp", VOCAB_AXES)),
        check_vma=False)
```

profile of v0, /device:TPU:0, one launch (start us, length us, event | category | flops | bytes accessed | tf_op | source)
XLA Modules:
  0.0 1446.1 jit_solution(1912743897414178065)
XLA Ops:
  0.6 117.2 %copy.12 = f32[1,24,128256]{1,0,2:T(1,128)} copy(f32[1,24,128256]{2,1,0:T(8,128)} %param.8) | data formatting | bytes 24625152 | tf_op args[2]
  117.9 0.5 broadcast.76
  118.4 560.6 %reduce = f32[128256,24]{1,0:T(8,128)} reduce(f32[128256,1,24]{2,1,0:T(1,128)} %bitcast.49, f32[]{:T(128)} %broadcast.76), dimensions={1}, to_apply=%bitcast.42.reduce_sub_computation | reduce | bytes 24625156
  678.9 55.2 %reshape.62 = f32[16,1,192384]{2,1,0:T(1,128)} reshape(f32[128256,24]{1,0:T(8,128)} %reduce) | data formatting | bytes 24625152
  734.2 7.8 all-to-all-start
  742.0 0.0 copy-done.2
  742.1 0.7 reshape.51
  742.8 0.0 copy-done.5
  742.8 34.0 %multiply_reduce_fusion = (f32[16,25]{1,0:T(8,128)S(1)}, f32[16,25,8016]{2,1,0:T(8,128)}) fusion(bf16[3072,8016]{0,1:T(8,128)(2,1)} %param.7, bf16[16,25,3072]{2,0,1:T(8,128)(2,1)S(1)} %copy-done.5), kind=kOutput, calls=%fused_computation.5 | convolution fusion | flops 19706533888 | bytes 64535104 | tf_op jit(solution)/shard_map/bgd,dv->bgv/dot_general | solution.py:16
  776.8 211.9 %pmax.7 = f32[16,25]{1,0:T(8,128)S(1)} all-reduce(f32[16,25]{1,0:T(8,128)S(1)} %get-tuple-element.12), channel_id=1, replica_groups=mesh['dp'=2,'tpa'=4,'tpb'=4] {'tpa','tpb'}, use_global_device_ids=true, to_apply=%region_1.0 | all-reduce | flops 400 | bytes 3200 | tf_op jit(solution)/shard_map/pmax | solution.py:17
  988.8 8.6 fusion.3
  997.4 64.3 %psum.14 = f32[16,25]{1,0:T(8,128)S(1)} all-reduce(f32[16,25]{1,0:T(8,128)S(1)} %fusion.3), channel_id=1, replica_groups=mesh['dp'=2,'tpa'=4,'tpb'=4] {'tpa','tpb'}, use_global_device_ids=true, to_apply=%region_3.0 | all-reduce | flops 400 | bytes 3200 | tf_op jit(solution)/shard_map/psum | solution.py:19
  1061.7 7.4 fusion.2
  1069.1 0.0 copy-start
  1069.1 5.8 copy-done
  1074.9 0.3 slice.39
  1075.2 0.8 copy.23
  1076.0 0.0 all-to-all-done
  1076.0 36.4 %reduce.1 = f32[16,192384]{1,0:T(8,128)} reduce(f32[16,1,192384]{2,1,0:T(1,128)} %all-to-all-done, f32[]{:T(128)} %broadcast.76), dimensions={1}, to_apply=%all_to_all.13.reduce_sub_computation | reduce | bytes 24625156 | tf_op jit(solution)/shard_map/all_to_all | solution.py:21
  1112.5 196.5 %reshape.63 = f32[128256,1,24]{2,1,0:T(1,128)} reshape(f32[16,192384]{1,0:T(8,128)} %reduce.1) | data formatting | bytes 24625152
  1309.0 37.4 %copy.14 = f32[1,24,16,8016]{3,1,2,0:T(8,128)} copy(f32[1,24,16,8016]{1,3,2,0:T(8,128)} %bitcast.48) | data formatting | bytes 24625152 | tf_op jit(solution)/shard_map/all_to_all | solution.py:21
  1346.4 13.8 fusion.16
  1360.2 0.0 copy-done.1
  1360.2 6.6 gather_fusion
  1366.8 0.1 reshape.54
  1366.8 0.0 copy-done.3
  1366.9 6.5 gather_fusion.1
  1373.4 0.1 reshape.60
  1373.5 57.6 %psum.15 = f32[3,16,24]{2,1,0:T(8,128)S(1)} all-reduce(f32[3,16,24]{2,1,0:T(8,128)S(1)} %pad_maximum_fusion), channel_id=1, replica_groups=mesh['dp'=2,'tpa'=4,'tpb'=4] {'tpa','tpb'}, use_global_device_ids=true, to_apply=%region_5.7 | all-reduce | flops 1152 | bytes 9216 | tf_op jit(solution)/shard_map/psum | solution.py:30
  1431.1 13.7 broadcast_divide_fusion
  1444.8 0.2 reduce_window.9
  1445.0 0.6 reduce_sum.29
  (15 shorter events, 0.1 us)
Async XLA Ops:
  734.2 7.9 copy-start.2
  734.2 8.6 copy-start.5
  734.2 341.9 %all-to-all-start = ((f32[16,1,192384]{2,1,0:T(1,128)}), f32[16,1,192384]{2,1,0:T(1,128)}, u32[]{:S(2)}, u32[]{:S(2)}) async-start(f32[16,1,192384]{2,1,0:T(1,128)} %reshape.62), calls=%async_computation | async-start | bytes 24625152 | tf_op jit(solution)/shard_map/all_to_all | solution.py:21
  1069.1 5.8 copy-start
  1346.4 13.8 copy-start.1
  1346.4 20.5 %copy-start.3 = (s32[16,24]{1,0:T(8,128)S(1)}, s32[16,24]{1,0:T(8,128)}, u32[]{:S(2)}) copy-start(s32[16,24]{1,0:T(8,128)} %param.9) | copy-start | bytes 4612
  1431.1 13.7 copy-start.4
where the time goes:
time: 1460 us; the launch traced here: 1450 us
  other arithmetic  641 us (44%)
  local copies, waits for them, and re-layouts  428 us (29%)
  blocking collectives  334 us (23%)
  matrix products  34 us (2%)
    unnamed x1, other arithmetic  561 us
    unnamed x17, local copies, waits for them, and re-layouts  376 us
    pmax x1, blocking collectives, local_step(): glob_max = lax.pmax(jnp.max(logits, axis=-1), VOCAB_AXES)  212 us
    psum x1, blocking collectives, local_step(): exp_sum = lax.psum(jnp.sum(exp_vals, axis=-1), VOCAB_AXES)  64.3 us
    psum x1, blocking collectives, local_step(): lax.psum(jnp.stack([p_pick, q_pick, jnp.sum(excess, axis=-1)]), VOCAB_AXES)  57.6 us
    all_to_all x1, local copies, waits for them, and re-layouts, local_step(): q_vocab = lax.all_to_all(q_draft, VOCAB_AXES, 2, 0, tiled=True)  37.4 us
    all_to_all x1, other arithmetic, local_step(): q_vocab = lax.all_to_all(q_draft, VOCAB_AXES, 2, 0, tiled=True)  36.4 us
    dot_general x1, matrix products, local_step(): jnp.einsum('bgd,dv->bgv', hidden, w_head, preferred_element_type=jnp.floa...  34 us
  transfers between devices with their start and end apart: 1, of which 0 were waited for; matrix products, arithmetic and copies ran while one was open for 4% of the time, Pallas kernels for 0%

commit v1 on v0

v1 whole, which is shorter than its diff:
```python
import functools

import jax
import jax.numpy as jnp
from jax import lax
from jax.experimental import pallas as pl
from jax.experimental.pallas import tpu as pltpu
from jax.sharding import PartitionSpec as P

INV_TEMP = 1.25
VOCAB_AXES = ("tpa", "tpb")
MESH = pl.DeviceIdType.MESH
LANES = 128
ROWS = 8
W_ROWS = 256
W_BUFS = 4


def xor4(a, r):
    low = lax.rem(lax.rem(a, 2) + lax.rem(r, 2), 2)
    high = lax.rem(lax.div(a, 2) + lax.div(r, 2), 2)
    return low + 2 * high


def exchange_kernel(n, phases, vl, hid_ref, w_ref, q_ref, x_ref, z_ref, tot_ref,
                    hid_v, hs, wbuf, qbuf, x_v, colmax, colsum, scale, part, stat, zmsg,
                    in_sem, w_sem, qs_sem, qr_sem, ss_sem, sr_sem, zs_sem, zr_sem):
    vp = z_ref.shape[1]
    tiles = vp // LANES
    last = vl - (tiles - 1) * LANES
    rows_all = z_ref.shape[0]
    draft_rows = phases * n * ROWS
    my_a, my_b = lax.axis_index("tpa"), lax.axis_index("tpb")
    me = my_a * 4 + my_b
    lane = lax.broadcasted_iota(jnp.int32, (ROWS, LANES), 1)

    def peer(r):
        return xor4(my_a, lax.div(r, 4)), xor4(my_b, lax.rem(r, 4))

    def window(k):
        col = lax.div(k * vl, LANES) * LANES
        return pl.multiple_of(col, LANES), k * vl - col

    def sized(k, body):
        _, o = window(k)
        wide = o + vl > vp
        pl.when(wide)(lambda: body(vp + LANES))
        pl.when(jnp.logical_not(wide))(lambda: body(vp))

    def q_copy(g, r, width):
        a, b = peer(r)
        col, _ = window(a * 4 + b)
        return pltpu.make_async_remote_copy(
            src_ref=q_ref.at[pl.ds(pl.multiple_of(g * ROWS, ROWS), ROWS), pl.ds(col, width)],
            dst_ref=qbuf.at[g, me, :, pl.ds(0, width)],
            send_sem=qs_sem.at[g, r], recv_sem=qr_sem.at[g, me],
            device_id={"tpa": a, "tpb": b}, device_id_type=MESH)

    def own_copy(g, width):
        col, _ = window(me)
        return pltpu.make_async_copy(
            q_ref.at[pl.ds(pl.multiple_of(g * ROWS, ROWS), ROWS), pl.ds(col, width)],
            qbuf.at[g, me, :, pl.ds(0, width)], qr_sem.at[g, me])

    def q_arrival(g, s, width):
        return pltpu.make_async_remote_copy(
            src_ref=qbuf.at[g, s, :, pl.ds(0, width)], dst_ref=qbuf.at[g, s, :, pl.ds(0, width)],
            send_sem=qs_sem.at[g, 0], recv_sem=qr_sem.at[g, s],
            device_id={"tpa": my_a, "tpb": my_b}, device_id_type=MESH)

    def send_phase(g):
        def one(r, c):
            a, b = peer(r)
            sized(a * 4 + b, lambda width: q_copy(g, r, width).start())
            return c
        lax.fori_loop(1, n, one, 0)

    def w_copy(c, slot):
        return pltpu.make_async_copy(w_ref.at[pl.ds(pl.multiple_of(c * W_ROWS, W_ROWS), W_ROWS), :], wbuf.at[slot], w_sem.at[slot])

    full_chunks = vl // W_ROWS
    w_tail = vl - full_chunks * W_ROWS
    tail_slot = full_chunks % W_BUFS
    tail_copy = pltpu.make_async_copy(
        w_ref.at[pl.ds(full_chunks * W_ROWS, w_tail), :], wbuf.at[tail_slot, pl.ds(0, w_tail), :], w_sem.at[tail_slot])

    hid_copy = pltpu.make_async_copy(hid_ref, hid_v, in_sem.at[0])
    x_copy = pltpu.make_async_copy(x_ref, x_v, in_sem.at[1])
    hid_copy.start()
    x_copy.start()
    for c in range(W_BUFS):
        w_copy(c, c).start()

    barrier = pltpu.get_barrier_semaphore()

    def greet(r, c):
        a, b = peer(r)
        pl.semaphore_signal(barrier, inc=1, device_id={"tpa": a, "tpb": b}, device_id_type=MESH)
        return c
    lax.fori_loop(1, n, greet, 0)
    pl.semaphore_wait(barrier, n - 1)

    send_phase(0)
    send_phase(1)
    for g in range(phases):
        sized(me, lambda width, g=g: own_copy(g, width).start())

    hid_copy.wait()
    row = lax.broadcasted_iota(jnp.int32, (rows_all, rows_all), 0)
    col = lax.broadcasted_iota(jnp.int32, (rows_all, rows_all), 1)
    source = jnp.where(row < draft_rows, ((row // (n * ROWS)) * ROWS + row % ROWS) * n + (row // ROWS) % n, row)
    permute = jnp.where(col == source, 1.0, 0.0).astype(jnp.bfloat16)
    depth = hid_v.shape[1]

    def permute_columns(c, carry):
        at = pl.ds(pl.multiple_of(c * 256, 256), 256)
        hs[:, at] = jnp.dot(permute, hid_v[:, at], preferred_element_type=jnp.float32).astype(jnp.bfloat16)
        return carry
    lax.fori_loop(0, depth // 256, permute_columns, 0)

    nt = (((1,), (1,)), ((), ()))

    def logits(c, carry):
        slot = lax.rem(c, W_BUFS)
        w_copy(c, slot).wait()
        z_ref[:, pl.ds(pl.multiple_of(c * W_ROWS, W_ROWS), W_ROWS)] = lax.dot_general(
            hs[...], wbuf[slot], nt, preferred_element_type=jnp.float32) * INV_TEMP

        @pl.when(c + W_BUFS < full_chunks)
        def _():
            w_copy(c + W_BUFS, slot).start()

        @pl.when(c + W_BUFS == full_chunks)
        def _():
            tail_copy.start()
        return carry
    lax.fori_loop(0, full_chunks, logits, 0)
    tail_copy.wait()
    z_ref[:, full_chunks * W_ROWS:vl] = lax.dot_general(
        hs[...], wbuf[tail_slot, 0:w_tail, :], nt, preferred_element_type=jnp.float32) * INV_TEMP

    def tile_of(j):
        return slice(j * LANES, (j + 1) * LANES)

    def row_stats(t, carry):
        rows = pl.ds(pl.multiple_of(t * ROWS, ROWS), ROWS)
        m = jnp.where(lane < last, z_ref[rows, tile_of(tiles - 1)], -jnp.inf)
        for j in range(tiles - 1):
            m = jnp.maximum(m, z_ref[rows, tile_of(j)])
        m = jnp.broadcast_to(jnp.max(m, axis=1, keepdims=True), (ROWS, LANES))
        s = jnp.zeros((ROWS, LANES), jnp.float32)
        for j in range(tiles):
            e = jnp.exp(z_ref[rows, tile_of(j)] - m)
            if j == tiles - 1:
                e = jnp.where(lane < last, e, 0.0)
            z_ref[rows, tile_of(j)] = e
            s = s + e
        colmax[rows, :] = m
        colsum[rows, :] = jnp.broadcast_to(jnp.sum(s, axis=1, keepdims=True), (ROWS, LANES))
        return carry
    lax.fori_loop(0, rows_all // ROWS, row_stats, 0)
    spare = colmax.shape[0] - rows_all
    colmax[rows_all:, :] = jnp.zeros((spare, LANES), jnp.float32)
    colsum[rows_all:, :] = jnp.ones((spare, LANES), jnp.float32)

    blocks = colmax.shape[0] // LANES

    def as_rows(ref):
        return jnp.concatenate([ref[i * LANES:(i + 1) * LANES, :].T[0:1, :] for i in range(blocks)], axis=0)
    stat[me, 0] = as_rows(colmax)
    stat[me, 1] = as_rows(colsum)

    def stat_copy(r, s):
        a, b = peer(r)
        return pltpu.make_async_remote_copy(
            src_ref=stat.at[me], dst_ref=stat.at[s], send_sem=ss_sem.at[r], recv_sem=sr_sem.at[s],
            device_id={"tpa": a, "tpb": b}, device_id_type=MESH)

    def send_stat(r, c):
        stat_copy(r, me).start()
        return c
    lax.fori_loop(1, n, send_stat, 0)
    send_phase(2)

    def wait_stat(r, c):
        a, b = peer(r)
        stat_copy(r, a * 4 + b).wait_recv()
        return c
    lax.fori_loop(1, n, wait_stat, 0)
    glob_max = stat[0, 0]
    for s in range(1, n):
        glob_max = jnp.maximum(glob_max, stat[s, 0])
    glob_sum = jnp.zeros_like(glob_max)
    for s in range(n):
        glob_sum = glob_sum + stat[s, 1] * jnp.exp(stat[s, 0] - glob_max)
    factor = jnp.exp(stat[me, 0] - glob_max) / glob_sum
    for i in range(blocks):
        scale[i * LANES:(i + 1) * LANES, :] = jnp.broadcast_to(factor[i:i + 1, :], (LANES, LANES)).T

    for t in range(draft_rows // ROWS, rows_all // ROWS):
        rows = slice(t * ROWS, (t + 1) * ROWS)
        for j in range(tiles):
            z_ref[rows, tile_of(j)] = z_ref[rows, tile_of(j)] * scale[rows, :]

    x_copy.wait()
    _, offset = window(me)
    shift = lax.rem(LANES - offset, LANES)
    lane_f = lane.astype(jnp.float32)
    num_draft = x_v.shape[1]

    def excess(g, s):
        rows = pl.ds(pl.multiple_of(g * (n * ROWS) + s * ROWS, ROWS), ROWS)
        tokens = jnp.broadcast_to(x_v[pl.ds(s, 1), :].astype(jnp.float32), (ROWS, num_draft))
        position = lax.broadcasted_iota(jnp.int32, (ROWS, num_draft), 0) + g * ROWS
        here = lax.broadcasted_iota(jnp.int32, (ROWS, num_draft), 1) == position
        token = jnp.sum(jnp.where(here, tokens, 0.0), axis=1, keepdims=True) - (me * vl).astype(jnp.float32)
        token = jnp.broadcast_to(jnp.where(token < vl, token, -1.0), (ROWS, LANES))
        sc = scale[rows, :]
        z_sum = p_pick = q_pick = jnp.zeros((ROWS, LANES), jnp.float32)
        this = pltpu.roll(qbuf[g, s, :, 0:LANES], shift, 1)
        for j in range(tiles):
            following = pltpu.roll(qbuf[g, s, :, (j + 1) * LANES:(j + 2) * LANES], shift, 1)
            q = jnp.where(lane < LANES - offset, this, following)
            this = following
            p = z_ref[rows, tile_of(j)] * sc
            d = jnp.maximum(p - q, 0.0)
            if j == tiles - 1:
                d = jnp.where(lane < last, d, 0.0)
            z_ref[rows, tile_of(j)] = d
            z_sum = z_sum + d
            hit = lane_f == token - float(j * LANES)
            p_pick = jnp.where(hit, p, p_pick)
            q_pick = jnp.where(hit, q, q_pick)
        part[0, rows, :] = z_sum
        part[1, rows, :] = p_pick
        part[2, rows, :] = q_pick

    def z_copy(g, r, s):
        a, b = peer(r)
        return pltpu.make_async_remote_copy(
            src_ref=zmsg.at[g, me], dst_ref=zmsg.at[g, s], send_sem=zs_sem.at[g, r], recv_sem=zr_sem.at[g, s],
            device_id={"tpa": a, "tpb": b}, device_id_type=MESH)

    def phase(g, carry):
        sized(me, lambda width: own_copy(g, width).wait())
        excess(g, me)

        def one(r, c):
            a, b = peer(r)
            s = a * 4 + b
            sized(me, lambda width: q_arrival(g, s, width).wait_recv())
            excess(g, s)
            return c
        lax.fori_loop(1, n, one, 0)
        block = pl.ds(pl.multiple_of(g * (n * ROWS), n * ROWS), n * ROWS)
        sums = [jnp.sum(part[i, block, :].T, axis=0, keepdims=True) for i in range(3)]
        zmsg[g, me] = jnp.concatenate(sums + [jnp.zeros((1, LANES), jnp.float32)], axis=0)

        def send(r, c):
            z_copy(g, r, me).start()
            return c
        lax.fori_loop(1, n, send, 0)
        return carry
    lax.fori_loop(0, phases, phase, 0)

    def collect(i, c):
        g, r = lax.div(i, n), lax.rem(i, n)

        @pl.when(r > 0)
        def _():
            a, b = peer(r)
            z_copy(g, r, a * 4 + b).wait_recv()
        return c
    lax.fori_loop(0, phases * n, collect, 0)
    for g in range(phases):
        total = zmsg[g, 0]
        for s in range(1, n):
            total = total + zmsg[g, s]
        tot_ref[g] = total

    def drain(i, c):
        g, r = lax.div(i, n), lax.rem(i, n)

        @pl.when(r > 0)
        def _():
            a, b = peer(r)
            sized(a * 4 + b, lambda width: q_copy(g, r, width).wait_send())
            z_copy(g, r, me).wait_send()

        @pl.when(jnp.logical_and(r > 0, g == 0))
        def _():
            stat_copy(r, me).wait_send()
        return c
    lax.fori_loop(0, phases * n, drain, 0)


def finish_kernel(n, phases, vl, tot_ref, z_ref, res_ref, bonus_ref, accept_ref, expected_ref, zcol):
    b = pl.program_id(0)
    width = n * ROWS
    num_draft = phases * ROWS

    @pl.when(b == 0)
    def _():
        for g in range(phases):
            zcol[g] = jnp.broadcast_to(tot_ref[g, 0:1, :], (width, LANES)).T
        bonus_ref[...] = z_ref[phases * width:phases * width + n, 0:vl]
        seq_of = lax.broadcasted_iota(jnp.int32, (n, width), 1) // ROWS == lax.broadcasted_iota(jnp.int32, (n, width), 0)
        pos_of = lax.broadcasted_iota(jnp.int32, (ROWS, width), 1) % ROWS == lax.broadcasted_iota(jnp.int32, (ROWS, width), 0)
        to_seq = (lax.broadcasted_iota(jnp.int32, (width, n), 0) // ROWS
                  == lax.broadcasted_iota(jnp.int32, (width, n), 1)).astype(jnp.float32)
        by_seq = jnp.zeros((n, num_draft), jnp.float32)
        by_pos = []
        for g in range(phases):
            a = jnp.minimum(1.0, tot_ref[g, 1:2, :] / tot_ref[g, 2:3, :])
            to_pos = (lax.broadcasted_iota(jnp.int32, (width, num_draft), 0) % ROWS + g * ROWS
                      == lax.broadcasted_iota(jnp.int32, (width, num_draft), 1)).astype(jnp.float32)
            by_seq = by_seq + jnp.dot(jnp.where(seq_of, jnp.broadcast_to(a, (n, width)), 0.0), to_pos,
                                      precision=lax.Precision.HIGHEST, preferred_element_type=jnp.float32)
            by_pos.append(jnp.dot(jnp.where(pos_of, jnp.broadcast_to(a, (ROWS, width)), 0.0), to_seq,
                                  precision=lax.Precision.HIGHEST, preferred_element_type=jnp.float32))
        accept_ref[...] = by_seq
        product = by_pos[0][0:1, :]
        total = product
        for k in range(1, num_draft):
            product = product * by_pos[k // ROWS][k % ROWS:k % ROWS + 1, :]
            total = total + product
        expected_ref[...] = total

    for g in range(phases):
        norm = zcol[g, pl.ds(pl.multiple_of(b * ROWS, ROWS), ROWS), :]
        rows = pl.ds(pl.multiple_of(g * width + b * ROWS, ROWS), ROWS)
        for j in range(pl.cdiv(vl, LANES)):
            w = min(LANES, vl - j * LANES)
            res_ref[0, g * ROWS:(g + 1) * ROWS, j * LANES:j * LANES + w] = (z_ref[rows, j * LANES:(j + 1) * LANES] / norm)[:, 0:w]


def solution(mesh):
    n = mesh.shape["tpa"] * mesh.shape["tpb"]

    def local_step(hidden, w_head, q_draft, x_draft):
        seqs, positions, depth = hidden.shape
        vl = w_head.shape[1]
        num_draft = x_draft.shape[1]
        phases = num_draft // ROWS
        vp = pl.cdiv(vl, LANES) * LANES
        rows = seqs * positions
        stat_rows = pl.cdiv(rows, LANES) * LANES
        f32 = jnp.float32
        any_spec = pl.BlockSpec(memory_space=pl.ANY)
        vmem_spec = pl.BlockSpec(memory_space=pltpu.VMEM)
        z, tot = pl.pallas_call(
            functools.partial(exchange_kernel, n, phases, vl),
            name="exchange",
            out_shape=(pltpu.VMEM((rows, vp), f32), pltpu.VMEM((phases, 4, LANES), f32)),
            in_specs=[any_spec] * 4,
            out_specs=(vmem_spec, vmem_spec),
            scratch_shapes=[
                pltpu.VMEM((rows, depth), jnp.bfloat16),
                pltpu.VMEM((rows, depth), jnp.bfloat16),
                pltpu.VMEM((W_BUFS, W_ROWS, depth), jnp.bfloat16),
                pltpu.VMEM((phases, n, ROWS, vp + LANES), f32),
                pltpu.VMEM((seqs, num_draft), jnp.int32),
                pltpu.VMEM((stat_rows, LANES), f32),
                pltpu.VMEM((stat_rows, LANES), f32),
                pltpu.VMEM((stat_rows, LANES), f32),
                pltpu.VMEM((3, phases * n * ROWS, LANES), f32),
                pltpu.VMEM((n, 2, stat_rows // LANES, LANES), f32),
                pltpu.VMEM((phases, n, 4, LANES), f32),
                pltpu.SemaphoreType.DMA((2,)),
                pltpu.SemaphoreType.DMA((W_BUFS,)),
                pltpu.SemaphoreType.DMA((phases, n)),
                pltpu.SemaphoreType.DMA((phases, n)),
                pltpu.SemaphoreType.DMA((n,)),
                pltpu.SemaphoreType.DMA((n,)),
                pltpu.SemaphoreType.DMA((phases, n)),
                pltpu.SemaphoreType.DMA((phases, n)),
            ],
            compiler_params=pltpu.CompilerParams(collective_id=0, has_side_effects=True, vmem_limit_bytes=48 * 2**20),
        )(hidden.transpose(1, 0, 2).reshape(rows, depth), w_head.T, q_draft.reshape(num_draft, q_draft.shape[2]), x_draft)
        residual, bonus, accept, expected = pl.pallas_call(
            functools.partial(finish_kernel, n, phases, vl),
            name="finish",
            grid=(seqs,),
            out_shape=(jax.ShapeDtypeStruct((seqs, num_draft, vl), f32), jax.ShapeDtypeStruct((seqs, vl), f32),
                       jax.ShapeDtypeStruct((seqs, num_draft), f32), jax.ShapeDtypeStruct((1, seqs), f32)),
            in_specs=[vmem_spec, vmem_spec],
            out_specs=(pl.BlockSpec((1, num_draft, vl), lambda b: (b, 0, 0)), pl.BlockSpec((seqs, vl), lambda b: (0, 0)),
                       pl.BlockSpec((seqs, num_draft), lambda b: (0, 0)), pl.BlockSpec((1, seqs), lambda b: (0, 0))),
            scratch_shapes=[pltpu.VMEM((phases, n * ROWS, LANES), f32)],
            compiler_params=pltpu.CompilerParams(vmem_limit_bytes=16 * 2**20),
        )(tot, z)
        return accept, expected.reshape(seqs), residual, bonus

    return jax.shard_map(
        local_step, mesh=mesh,
        in_specs=(P("dp", None, None), P(None, VOCAB_AXES), P(("dp",) + VOCAB_AXES, None, None), P("dp", None)),
        out_specs=(P("dp", None), P("dp"), P("dp", None, VOCAB_AXES), P("dp", VOCAB_AXES)),
        check_vma=False)
```

time: 1460 us -> 305 us (0.21)
  other arithmetic: 641 us -> 0 us
  local copies, waits for them, and re-layouts: 428 us -> 0 us
  blocking collectives: 334 us -> 0 us
  Pallas kernels: 0 us -> 304 us
  matrix products: 34 us -> 0 us
    unnamed x1 -> x0, other arithmetic: 561 us -> none
    unnamed x17 -> x0, local copies, waits for them, and re-layouts: 376 us -> none
    pallas_call x0 -> x2, Pallas kernels: none -> 304 us  [the longest x1 296 us: local_step(): pl.pallas_call(functools.partial(exchange_kernel, n, phases, vl), name='e...]
    pmax x1 -> x0, blocking collectives: 212 us -> none  [local_step(): glob_max = lax.pmax(jnp.max(logits, axis=-1), VOCAB_AXES)]
    psum x2 -> x0, blocking collectives: 122 us -> none  [the longest x1 64.3 us: local_step(): exp_sum = lax.psum(jnp.sum(exp_vals, axis=-1), VOCAB_AXES)]
    all_to_all x1 -> x0, local copies, waits for them, and re-layouts: 37.4 us -> none  [local_step(): q_vocab = lax.all_to_all(q_draft, VOCAB_AXES, 2, 0, tiled=True)]
    all_to_all x1 -> x0, other arithmetic: 36.4 us -> none  [local_step(): q_vocab = lax.all_to_all(q_draft, VOCAB_AXES, 2, 0, tiled=True)]
    dot_general x1 -> x0, matrix products: 34 us -> none  [local_step(): jnp.einsum('bgd,dv->bgv', hidden, w_head, preferred_element_type=jnp.floa...]
  transfers between devices with their start and end apart: 1 -> 0, of which waited for: 0 -> 0; matrix products, arithmetic and copies ran while one was open for 4% -> 0% of each run, Pallas kernels for 0% -> 0%
where the time goes in v1:
time: 305 us
  Pallas kernels  304 us (100%)
    pallas_call x1, Pallas kernels, local_step(): pl.pallas_call(functools.partial(exchange_kernel, n, phases, vl), name='e...  296 us
    pallas_call x1, Pallas kernels, local_step(): pl.pallas_call(functools.partial(finish_kernel, n, phases, vl), name='fin...  8.37 us

profile of v1, /device:TPU:0, one launch (start us, length us, event | category | flops | bytes accessed | tf_op | source)
XLA Modules:
  0.0 305.0 jit_solution(18299811484402833627)
XLA Ops:
  0.6 296.0 %exchange.1 = (f32[400,8064]{1,0:T(8,128)S(1)}, f32[3,4,128]{2,1,0:T(4,128)S(1)}) custom-call(bf16[400,3072]{1,0:T(8,128)(2,1)} %bitcast.8, bf16[8016,3072]{1,0:T(8,128)(2,1)} %bitcast.6, f32[24,128256]{1,0:T(8,128)} %bitcast.7, s32[16,24]{1,0:T(8,128)} %x_ref.1), custom_call_target="tpu_custom_call" | custom-call | tf_op jit(solution)/shard_map/exchange/pallas_call | solution.py:351
  296.7 8.4 %finish.1 = (f32[16,24,8016]{2,1,0:T(8,128)}, f32[16,8016]{1,0:T(8,128)}, f32[16,24]{1,0:T(8,128)}, f32[1,16]{1,0:T(1,128)}) custom-call(f32[3,4,128]{2,1,0:T(4,128)S(1)} %get-tuple-element.10.tot_ref, f32[400,8064]{1,0:T(8,128)S(1)} %get-tuple-element.11.z_ref), custom_call_target="tpu_custom_call" | custom-call | tf_op jit(solution)/shard_map/finish/pallas_call | solution.py:380

commit v2 on v1

--- a/solution.py
+++ b/solution.py
@@ -14,6 +14,9 @@
 ROWS = 8
 W_ROWS = 256
 W_BUFS = 4
+ORDER_0 = (8, 12, 4, 9, 13, 1, 10, 14, 5, 11, 15, 2, 6, 7, 3)
+ORDER_1 = (12, 4, 8, 13, 1, 9, 14, 5, 10, 15, 2, 11, 6, 7, 3)
+SCALE = 2.0 ** 64
 
 
 def xor4(a, r):
@@ -68,12 +71,17 @@
             send_sem=qs_sem.at[g, 0], recv_sem=qr_sem.at[g, s],
             device_id={"tpa": my_a, "tpb": my_b}, device_id_type=MESH)
 
+    core = lax.rem(my_b, 2)
+
+    def nth(g, i):
+        i = i if g < phases - 1 else len(ORDER_0) - 1 - i
+        return ORDER_0[i] + core * (ORDER_1[i] - ORDER_0[i])
+
     def send_phase(g):
-        def one(r, c):
+        for i in range(n - 1):
+            r = nth(g, i)
             a, b = peer(r)
-            sized(a * 4 + b, lambda width: q_copy(g, r, width).start())
-            return c
-        lax.fori_loop(1, n, one, 0)
+            sized(a * 4 + b, lambda width, r=r: q_copy(g, r, width).start())
 
     def w_copy(c, slot):
         return pltpu.make_async_copy(w_ref.at[pl.ds(pl.multiple_of(c * W_ROWS, W_ROWS), W_ROWS), :], wbuf.at[slot], w_sem.at[slot])
@@ -245,7 +253,8 @@
         sized(me, lambda width: own_copy(g, width).wait())
         excess(g, me)
 
-        def one(r, c):
+        def one(i, c):
+            r = jnp.where(g == phases - 1, i, n - i)
             a, b = peer(r)
             s = a * 4 + b
             sized(me, lambda width: q_arrival(g, s, width).wait_recv())
@@ -263,12 +272,27 @@
         return carry
     lax.fori_loop(0, phases, phase, 0)
 
-    def collect(i, c):
+    def drain(i, c):
         g, r = lax.div(i, n), lax.rem(i, n)
 
         @pl.when(r > 0)
         def _():
             a, b = peer(r)
+            sized(a * 4 + b, lambda width: q_copy(g, r, width).wait_send())
+
+        @pl.when(jnp.logical_and(r > 0, g == 0))
+        def _():
+            stat_copy(r, me).wait_send()
+        return c
+    lax.fori_loop(0, phases * n, drain, 0)
+
+    def collect(i, c):
+        g, r = lax.div(i, n), lax.rem(i, n)
+
+        @pl.when(r > 0)
+        def _():
+            a, b = peer(r)
+            z_copy(g, r, me).wait_send()
             z_copy(g, r, a * 4 + b).wait_recv()
         return c
     lax.fori_loop(0, phases * n, collect, 0)
@@ -278,60 +302,58 @@
             total = total + zmsg[g, s]
         tot_ref[g] = total
 
-    def drain(i, c):
-        g, r = lax.div(i, n), lax.rem(i, n)
-
-        @pl.when(r > 0)
-        def _():
-            a, b = peer(r)
-            sized(a * 4 + b, lambda width: q_copy(g, r, width).wait_send())
-            z_copy(g, r, me).wait_send()
-
-        @pl.when(jnp.logical_and(r > 0, g == 0))
-        def _():
-            stat_copy(r, me).wait_send()
-        return c
-    lax.fori_loop(0, phases * n, drain, 0)
-
-
-def finish_kernel(n, phases, vl, tot_ref, z_ref, res_ref, bonus_ref, accept_ref, expected_ref, zcol):
-    b = pl.program_id(0)
+
+def finish_kernel(n, phases, vl, tot_ref, z_ref, res_ref, bonus_ref, accept_ref, expected_ref, inverse, staged, staged_bonus, sem, bonus_sem):
     width = n * ROWS
     num_draft = phases * ROWS
-
-    @pl.when(b == 0)
-    def _():
+    for g in range(phases):
+        inverse[g] = jnp.broadcast_to(1.0 / (tot_ref[g, 0:1, :] * SCALE), (width, LANES)).T
+
+    def block_copy(b):
+        return pltpu.make_async_copy(staged.at[b], res_ref.at[b], sem.at[b])
+
+    def one(b, c):
         for g in range(phases):
-            zcol[g] = jnp.broadcast_to(tot_ref[g, 0:1, :], (width, LANES)).T
-        bonus_ref[...] = z_ref[phases * width:phases * width + n, 0:vl]
-        seq_of = lax.broadcasted_iota(jnp.int32, (n, width), 1) // ROWS == lax.broadcasted_iota(jnp.int32, (n, width), 0)
-        pos_of = lax.broadcasted_iota(jnp.int32, (ROWS, width), 1) % ROWS == lax.broadcasted_iota(jnp.int32, (ROWS, width), 0)
-        to_seq = (lax.broadcasted_iota(jnp.int32, (width, n), 0) // ROWS
-                  == lax.broadcasted_iota(jnp.int32, (width, n), 1)).astype(jnp.float32)
-        by_seq = jnp.zeros((n, num_draft), jnp.float32)
-        by_pos = []
-        for g in range(phases):
-            a = jnp.minimum(1.0, tot_ref[g, 1:2, :] / tot_ref[g, 2:3, :])
-            to_pos = (lax.broadcasted_iota(jnp.int32, (width, num_draft), 0) % ROWS + g * ROWS
-                      == lax.broadcasted_iota(jnp.int32, (width, num_draft), 1)).astype(jnp.float32)
-            by_seq = by_seq + jnp.dot(jnp.where(seq_of, jnp.broadcast_to(a, (n, width)), 0.0), to_pos,
-                                      precision=lax.Precision.HIGHEST, preferred_element_type=jnp.float32)
-            by_pos.append(jnp.dot(jnp.where(pos_of, jnp.broadcast_to(a, (ROWS, width)), 0.0), to_seq,
-                                  precision=lax.Precision.HIGHEST, preferred_element_type=jnp.float32))
-        accept_ref[...] = by_seq
-        product = by_pos[0][0:1, :]
-        total = product
-        for k in range(1, num_draft):
-            product = product * by_pos[k // ROWS][k % ROWS:k % ROWS + 1, :]
-            total = total + product
-        expected_ref[...] = total
-
+            inv = inverse[g, pl.ds(pl.multiple_of(b * ROWS, ROWS), ROWS), :]
+            rows = pl.ds(pl.multiple_of(g * width + b * ROWS, ROWS), ROWS)
+            for j in range(pl.cdiv(vl, LANES)):
+                w = min(LANES, vl - j * LANES)
+                value = (z_ref[rows, j * LANES:(j + 1) * LANES] * SCALE) * inv
+                staged[b, g * ROWS:(g + 1) * ROWS, j * LANES:j * LANES + w] = value[:, 0:w]
+        block_copy(b).start()
+        return c
+    lax.fori_loop(0, n, one, 0)
+    staged_bonus[...] = z_ref[phases * width:phases * width + n, 0:vl]
+    bonus_copy = pltpu.make_async_copy(staged_bonus, bonus_ref, bonus_sem)
+    bonus_copy.start()
+
+    seq_of = lax.broadcasted_iota(jnp.int32, (n, width), 1) // ROWS == lax.broadcasted_iota(jnp.int32, (n, width), 0)
+    pos_of = lax.broadcasted_iota(jnp.int32, (ROWS, width), 1) % ROWS == lax.broadcasted_iota(jnp.int32, (ROWS, width), 0)
+    to_seq = (lax.broadcasted_iota(jnp.int32, (width, n), 0) // ROWS
+              == lax.broadcasted_iota(jnp.int32, (width, n), 1)).astype(jnp.float32)
+    by_seq = jnp.zeros((n, num_draft), jnp.float32)
+    by_pos = []
     for g in range(phases):
-        norm = zcol[g, pl.ds(pl.multiple_of(b * ROWS, ROWS), ROWS), :]
-        rows = pl.ds(pl.multiple_of(g * width + b * ROWS, ROWS), ROWS)
-        for j in range(pl.cdiv(vl, LANES)):
-            w = min(LANES, vl - j * LANES)
-            res_ref[0, g * ROWS:(g + 1) * ROWS, j * LANES:j * LANES + w] = (z_ref[rows, j * LANES:(j + 1) * LANES] / norm)[:, 0:w]
+        a = jnp.minimum(1.0, tot_ref[g, 1:2, :] / tot_ref[g, 2:3, :])
+        to_pos = (lax.broadcasted_iota(jnp.int32, (width, num_draft), 0) % ROWS + g * ROWS
+                  == lax.broadcasted_iota(jnp.int32, (width, num_draft), 1)).astype(jnp.float32)
+        by_seq = by_seq + jnp.dot(jnp.where(seq_of, jnp.broadcast_to(a, (n, width)), 0.0), to_pos,
+                                  precision=lax.Precision.HIGHEST, preferred_element_type=jnp.float32)
+        by_pos.append(jnp.dot(jnp.where(pos_of, jnp.broadcast_to(a, (ROWS, width)), 0.0), to_seq,
+                              precision=lax.Precision.HIGHEST, preferred_element_type=jnp.float32))
+    accept_ref[...] = by_seq
+    product = by_pos[0][0:1, :]
+    total = product
+    for k in range(1, num_draft):
+        product = product * by_pos[k // ROWS][k % ROWS:k % ROWS + 1, :]
+        total = total + product
+    expected_ref[...] = total
+
+    def finished(b, c):
+        block_copy(b).wait()
+        return c
+    lax.fori_loop(0, n, finished, 0)
+    bonus_copy.wait()
 
 
 def solution(mesh):
@@ -380,14 +402,13 @@
         residual, bonus, accept, expected = pl.pallas_call(
             functools.partial(finish_kernel, n, phases, vl),
             name="finish",
-            grid=(seqs,),
             out_shape=(jax.ShapeDtypeStruct((seqs, num_draft, vl), f32), jax.ShapeDtypeStruct((seqs, vl), f32),
                        jax.ShapeDtypeStruct((seqs, num_draft), f32), jax.ShapeDtypeStruct((1, seqs), f32)),
             in_specs=[vmem_spec, vmem_spec],
-            out_specs=(pl.BlockSpec((1, num_draft, vl), lambda b: (b, 0, 0)), pl.BlockSpec((seqs, vl), lambda b: (0, 0)),
-                       pl.BlockSpec((seqs, num_draft), lambda b: (0, 0)), pl.BlockSpec((1, seqs), lambda b: (0, 0))),
-            scratch_shapes=[pltpu.VMEM((phases, n * ROWS, LANES), f32)],
-            compiler_params=pltpu.CompilerParams(vmem_limit_bytes=16 * 2**20),
+            out_specs=(any_spec, any_spec, vmem_spec, vmem_spec),
+            scratch_shapes=[pltpu.VMEM((phases, n * ROWS, LANES), f32), pltpu.VMEM((seqs, num_draft, vl), f32),
+                            pltpu.VMEM((seqs, vl), f32), pltpu.SemaphoreType.DMA((seqs,)), pltpu.SemaphoreType.DMA],
+            compiler_params=pltpu.CompilerParams(vmem_limit_bytes=32 * 2**20),
         )(tot, z)
         return accept, expected.reshape(seqs), residual, bonus
 

time: 305 us -> 294 us (0.964)
  Pallas kernels: 304 us -> 293 us
    pallas_call x1, Pallas kernels: 296 us -> 287 us  [local_step(): pl.pallas_call(functools.partial(exchange_kernel, n, phases, vl), name='e...]
where the time goes in v2:
time: 294 us
  Pallas kernels  293 us (100%)
    pallas_call x1, Pallas kernels, local_step(): pl.pallas_call(functools.partial(exchange_kernel, n, phases, vl), name='e...  287 us

profile of v2, /device:TPU:0, one launch (start us, length us, event | category | flops | bytes accessed | tf_op | source)
XLA Modules:
  0.0 293.7 jit_solution(16944840597115223327)
XLA Ops:
  0.6 287.4 %exchange.1 = (f32[400,8064]{1,0:T(8,128)S(1)}, f32[3,4,128]{2,1,0:T(4,128)S(1)}) custom-call(bf16[400,3072]{1,0:T(8,128)(2,1)} %bitcast.8, bf16[8016,3072]{1,0:T(8,128)(2,1)} %bitcast.6, f32[24,128256]{1,0:T(8,128)} %bitcast.7, s32[16,24]{1,0:T(8,128)} %x_ref.1), custom_call_target="tpu_custom_call" | custom-call | tf_op jit(solution)/shard_map/exchange/pallas_call | solution.py:373
  288.1 5.6 %finish.1 = (f32[16,24,8016]{2,1,0:T(8,128)}, f32[16,8016]{1,0:T(8,128)}, f32[16,24]{1,0:T(8,128)}, f32[1,16]{1,0:T(1,128)}) custom-call(f32[3,4,128]{2,1,0:T(4,128)S(1)} %get-tuple-element.10.tot_ref, f32[400,8064]{1,0:T(8,128)S(1)} %get-tuple-element.11.z_ref), custom_call_target="tpu_custom_call" | custom-call | tf_op jit(solution)/shard_map/finish/pallas_call | solution.py:402

commit v3 on v2

--- a/solution.py
+++ b/solution.py
@@ -14,8 +14,6 @@
 ROWS = 8
 W_ROWS = 256
 W_BUFS = 4
-ORDER_0 = (8, 12, 4, 9, 13, 1, 10, 14, 5, 11, 15, 2, 6, 7, 3)
-ORDER_1 = (12, 4, 8, 13, 1, 9, 14, 5, 10, 15, 2, 11, 6, 7, 3)
 SCALE = 2.0 ** 64
 
 
@@ -26,8 +24,8 @@
 
 
 def exchange_kernel(n, phases, vl, hid_ref, w_ref, q_ref, x_ref, z_ref, tot_ref,
-                    hid_v, hs, wbuf, qbuf, x_v, colmax, colsum, scale, part, stat, zmsg,
-                    in_sem, w_sem, qs_sem, qr_sem, ss_sem, sr_sem, zs_sem, zr_sem):
+                    hid_v, hs, wbuf, sbuf, qbuf, x_v, colmax, colsum, scale, part, stat, zmsg,
+                    in_sem, w_sem, ld_sem, qs_sem, qr_sem, ss_sem, sr_sem, zs_sem, zr_sem):
     vp = z_ref.shape[1]
     tiles = vp // LANES
     last = vl - (tiles - 1) * LANES
@@ -50,38 +48,78 @@
         pl.when(wide)(lambda: body(vp + LANES))
         pl.when(jnp.logical_not(wide))(lambda: body(vp))
 
-    def q_copy(g, r, width):
+    core = lax.rem(my_b, 2)
+
+    def nth(i):
+        r = lax.rem((n // 2 + 1) * i + n // 2, n)
+        far = lax.div(r, n // 2)
+        return far * (n // 2 + lax.rem(r + core * (n // 4), n // 2)) + (1 - far) * r
+
+    def width_of(g):
+        return vp if g < phases - 1 else vp - LANES
+
+    def load(g, k, width):
+        col, _ = window(k)
+        return pltpu.make_async_copy(q_ref.at[g * ROWS:(g + 1) * ROWS, pl.ds(col, width)], sbuf.at[g, k, :, pl.ds(0, width)], ld_sem.at[g, k])
+
+    def q_copy(g, r, s):
         a, b = peer(r)
-        col, _ = window(a * 4 + b)
         return pltpu.make_async_remote_copy(
-            src_ref=q_ref.at[pl.ds(pl.multiple_of(g * ROWS, ROWS), ROWS), pl.ds(col, width)],
-            dst_ref=qbuf.at[g, me, :, pl.ds(0, width)],
-            send_sem=qs_sem.at[g, r], recv_sem=qr_sem.at[g, me],
+            src_ref=sbuf.at[g, a * 4 + b, :, pl.ds(0, width_of(g))], dst_ref=qbuf.at[g, s, :, pl.ds(0, width_of(g))],
+            send_sem=qs_sem.at[g, r], recv_sem=qr_sem.at[g, s],
             device_id={"tpa": a, "tpb": b}, device_id_type=MESH)
 
-    def own_copy(g, width):
-        col, _ = window(me)
-        return pltpu.make_async_copy(
-            q_ref.at[pl.ds(pl.multiple_of(g * ROWS, ROWS), ROWS), pl.ds(col, width)],
-            qbuf.at[g, me, :, pl.ds(0, width)], qr_sem.at[g, me])
-
-    def q_arrival(g, s, width):
-        return pltpu.make_async_remote_copy(
-            src_ref=qbuf.at[g, s, :, pl.ds(0, width)], dst_ref=qbuf.at[g, s, :, pl.ds(0, width)],
-            send_sem=qs_sem.at[g, 0], recv_sem=qr_sem.at[g, s],
-            device_id={"tpa": my_a, "tpb": my_b}, device_id_type=MESH)
-
-    core = lax.rem(my_b, 2)
-
-    def nth(g, i):
-        i = i if g < phases - 1 else len(ORDER_0) - 1 - i
-        return ORDER_0[i] + core * (ORDER_1[i] - ORDER_0[i])
+    def tile_of(j):
+        return slice(j * LANES, (j + 1) * LANES)
+
+    free = LANES - last
+
+    def prepare(g, k):
+        _, o = window(k)
+        shift = lax.rem(LANES - o, LANES)
+
+        def last_tile(h):
+            return jnp.where(lane < LANES - o, pltpu.roll(sbuf[h, k, :, tile_of(tiles - 1)], shift, 1),
+                             pltpu.roll(sbuf[h, k, :, tile_of(tiles)], shift, 1))
+        ending = last_tile(g)
+        if g < phases - 1:
+            guest = pltpu.roll(last_tile(phases - 1), last if g == 0 else LANES - (free - last) % LANES, 1)
+            ending = jnp.where(lane < last, ending, guest)
+        this = pltpu.roll(sbuf[g, k, :, tile_of(0)], shift, 1)
+        for j in range(tiles - 1):
+            following = pltpu.roll(sbuf[g, k, :, tile_of(j + 1)], shift, 1)
+            sbuf[g, k, :, tile_of(j)] = jnp.where(lane < LANES - o, this, following)
+            this = following
+        sbuf[g, k, :, tile_of(tiles - 1)] = ending
 
     def send_phase(g):
-        for i in range(n - 1):
-            r = nth(g, i)
-            a, b = peer(r)
-            sized(a * 4 + b, lambda width, r=r: q_copy(g, r, width).start())
+        def one(i, c):
+            @pl.when(i < n)
+            def _():
+                r = nth(i)
+                a, b = peer(r)
+                k = a * 4 + b
+                if g == 0:
+                    sized(k, lambda width: load(0, k, width).wait())
+                    sized(k, lambda width: load(phases - 1, k, width).wait())
+                elif g < phases - 1:
+                    sized(k, lambda width: load(g, k, width).wait())
+                prepare(g, k)
+
+                @pl.when(r == 0)
+                def _():
+                    for j in range(tiles):
+                        qbuf[g, me, :, tile_of(j)] = sbuf[g, me, :, tile_of(j)]
+
+            @pl.when(i > 0)
+            def _():
+                before = nth(i - 1)
+
+                @pl.when(before > 0)
+                def _():
+                    q_copy(g, before, me).start()
+            return c
+        lax.fori_loop(0, n + 1, one, 0)
 
     def w_copy(c, slot):
         return pltpu.make_async_copy(w_ref.at[pl.ds(pl.multiple_of(c * W_ROWS, W_ROWS), W_ROWS), :], wbuf.at[slot], w_sem.at[slot])
@@ -94,6 +132,17 @@
 
     hid_copy = pltpu.make_async_copy(hid_ref, hid_v, in_sem.at[0])
     x_copy = pltpu.make_async_copy(x_ref, x_v, in_sem.at[1])
+    def start_load(g):
+        def one(i, c):
+            a, b = peer(nth(i))
+            k = a * 4 + b
+            sized(k, lambda width: load(g, k, width).start())
+            if g == 0:
+                sized(k, lambda width: load(phases - 1, k, width).start())
+            return c
+        lax.fori_loop(0, n, one, 0)
+    for g in range(phases - 1):
+        start_load(g)
     hid_copy.start()
     x_copy.start()
     for c in range(W_BUFS):
@@ -110,8 +159,6 @@
 
     send_phase(0)
     send_phase(1)
-    for g in range(phases):
-        sized(me, lambda width, g=g: own_copy(g, width).start())
 
     hid_copy.wait()
     row = lax.broadcasted_iota(jnp.int32, (rows_all, rows_all), 0)
@@ -146,9 +193,6 @@
     tail_copy.wait()
     z_ref[:, full_chunks * W_ROWS:vl] = lax.dot_general(
         hs[...], wbuf[tail_slot, 0:w_tail, :], nt, preferred_element_type=jnp.float32) * INV_TEMP
-
-    def tile_of(j):
-        return slice(j * LANES, (j + 1) * LANES)
 
     def row_stats(t, carry):
         rows = pl.ds(pl.multiple_of(t * ROWS, ROWS), ROWS)
@@ -211,8 +255,6 @@
             z_ref[rows, tile_of(j)] = z_ref[rows, tile_of(j)] * scale[rows, :]
 
     x_copy.wait()
-    _, offset = window(me)
-    shift = lax.rem(LANES - offset, LANES)
     lane_f = lane.astype(jnp.float32)
     num_draft = x_v.shape[1]
 
@@ -225,11 +267,12 @@
         token = jnp.broadcast_to(jnp.where(token < vl, token, -1.0), (ROWS, LANES))
         sc = scale[rows, :]
         z_sum = p_pick = q_pick = jnp.zeros((ROWS, LANES), jnp.float32)
-        this = pltpu.roll(qbuf[g, s, :, 0:LANES], shift, 1)
         for j in range(tiles):
-            following = pltpu.roll(qbuf[g, s, :, (j + 1) * LANES:(j + 2) * LANES], shift, 1)
-            q = jnp.where(lane < LANES - offset, this, following)
-            this = following
+            if g == phases - 1 and j == tiles - 1:
+                q = jnp.where(lane < free, pltpu.roll(qbuf[0, s, :, tile_of(j)], free, 1),
+                              pltpu.roll(qbuf[1, s, :, tile_of(j)], (free - last) % LANES, 1))
+            else:
+                q = qbuf[g, s, :, tile_of(j)]
             p = z_ref[rows, tile_of(j)] * sc
             d = jnp.maximum(p - q, 0.0)
             if j == tiles - 1:
@@ -249,58 +292,46 @@
             src_ref=zmsg.at[g, me], dst_ref=zmsg.at[g, s], send_sem=zs_sem.at[g, r], recv_sem=zr_sem.at[g, s],
             device_id={"tpa": a, "tpb": b}, device_id_type=MESH)
 
-    def phase(g, carry):
-        sized(me, lambda width: own_copy(g, width).wait())
-        excess(g, me)
-
-        def one(i, c):
-            r = jnp.where(g == phases - 1, i, n - i)
+    def add_up(g):
+        def arrived(r, c):
             a, b = peer(r)
-            s = a * 4 + b
-            sized(me, lambda width: q_arrival(g, s, width).wait_recv())
-            excess(g, s)
+            z_copy(g, r, a * 4 + b).wait_recv()
             return c
-        lax.fori_loop(1, n, one, 0)
-        block = pl.ds(pl.multiple_of(g * (n * ROWS), n * ROWS), n * ROWS)
-        sums = [jnp.sum(part[i, block, :].T, axis=0, keepdims=True) for i in range(3)]
-        zmsg[g, me] = jnp.concatenate(sums + [jnp.zeros((1, LANES), jnp.float32)], axis=0)
-
-        def send(r, c):
-            z_copy(g, r, me).start()
-            return c
-        lax.fori_loop(1, n, send, 0)
-        return carry
-    lax.fori_loop(0, phases, phase, 0)
-
-    def drain(i, c):
-        g, r = lax.div(i, n), lax.rem(i, n)
-
-        @pl.when(r > 0)
-        def _():
-            a, b = peer(r)
-            sized(a * 4 + b, lambda width: q_copy(g, r, width).wait_send())
-
-        @pl.when(jnp.logical_and(r > 0, g == 0))
-        def _():
-            stat_copy(r, me).wait_send()
-        return c
-    lax.fori_loop(0, phases * n, drain, 0)
-
-    def collect(i, c):
-        g, r = lax.div(i, n), lax.rem(i, n)
-
-        @pl.when(r > 0)
-        def _():
-            a, b = peer(r)
-            z_copy(g, r, me).wait_send()
-            z_copy(g, r, a * 4 + b).wait_recv()
-        return c
-    lax.fori_loop(0, phases * n, collect, 0)
-    for g in range(phases):
+        lax.fori_loop(1, n, arrived, 0)
         total = zmsg[g, 0]
         for s in range(1, n):
             total = total + zmsg[g, s]
         tot_ref[g] = total
+
+    for g in range(phases):
+        def one(i, c, g=g):
+            r = nth(i)
+            a, b = peer(r)
+            s = a * 4 + b
+
+            @pl.when(r > 0)
+            def _():
+                q_copy(g, r, s).wait_recv()
+            excess(g, s)
+            return c
+        lax.fori_loop(0, n, one, 0)
+        block = slice(g * n * ROWS, (g + 1) * n * ROWS)
+        zmsg[g, me] = jnp.concatenate([jnp.sum(part[i, block, :].T, axis=0, keepdims=True) for i in range(3)], axis=0)
+
+        def send(r, c, g=g):
+            z_copy(g, r, me).start()
+            return c
+        lax.fori_loop(1, n, send, 0)
+
+    def drain(r, c):
+        for g in range(phases):
+            q_copy(g, r, me).wait_send()
+            z_copy(g, r, me).wait_send()
+        stat_copy(r, me).wait_send()
+        return c
+    lax.fori_loop(1, n, drain, 0)
+    for g in range(phases):
+        add_up(g)
 
 
 def finish_kernel(n, phases, vl, tot_ref, z_ref, res_ref, bonus_ref, accept_ref, expected_ref, inverse, staged, staged_bonus, sem, bonus_sem):
@@ -373,7 +404,7 @@
         z, tot = pl.pallas_call(
             functools.partial(exchange_kernel, n, phases, vl),
             name="exchange",
-            out_shape=(pltpu.VMEM((rows, vp), f32), pltpu.VMEM((phases, 4, LANES), f32)),
+            out_shape=(pltpu.VMEM((rows, vp), f32), pltpu.VMEM((phases, 3, LANES), f32)),
             in_specs=[any_spec] * 4,
             out_specs=(vmem_spec, vmem_spec),
             scratch_shapes=[
@@ -381,15 +412,17 @@
                 pltpu.VMEM((rows, depth), jnp.bfloat16),
                 pltpu.VMEM((W_BUFS, W_ROWS, depth), jnp.bfloat16),
                 pltpu.VMEM((phases, n, ROWS, vp + LANES), f32),
+                pltpu.VMEM((phases, n, ROWS, vp), f32),
                 pltpu.VMEM((seqs, num_draft), jnp.int32),
                 pltpu.VMEM((stat_rows, LANES), f32),
                 pltpu.VMEM((stat_rows, LANES), f32),
                 pltpu.VMEM((stat_rows, LANES), f32),
                 pltpu.VMEM((3, phases * n * ROWS, LANES), f32),
                 pltpu.VMEM((n, 2, stat_rows // LANES, LANES), f32),
-                pltpu.VMEM((phases, n, 4, LANES), f32),
+                pltpu.VMEM((phases, n, 3, LANES), f32),
                 pltpu.SemaphoreType.DMA((2,)),
                 pltpu.SemaphoreType.DMA((W_BUFS,)),
+                pltpu.SemaphoreType.DMA((phases, n)),
                 pltpu.SemaphoreType.DMA((phases, n)),
                 pltpu.SemaphoreType.DMA((phases, n)),
                 pltpu.SemaphoreType.DMA((n,)),

time: 294 us -> 292 us (level)
  no operation moved by 1% of the time
where the time goes in v3:
time: 292 us
  Pallas kernels  291 us (100%)
    pallas_call x1, Pallas kernels, local_step(): pl.pallas_call(functools.partial(exchange_kernel, n, phases, vl), name='e...  285 us

profile of v3, /device:TPU:0, one launch (start us, length us, event | category | flops | bytes accessed | tf_op | source)
XLA Modules:
  0.0 291.5 jit_solution(2902393599201366850)
XLA Ops:
  0.6 285.3 %exchange.1 = (f32[400,8064]{1,0:T(8,128)S(1)}, f32[3,3,128]{2,1,0:T(4,128)S(1)}) custom-call(bf16[400,3072]{1,0:T(8,128)(2,1)} %bitcast.8, bf16[8016,3072]{1,0:T(8,128)(2,1)} %bitcast.6, f32[24,128256]{1,0:T(8,128)} %bitcast.7, s32[16,24]{1,0:T(8,128)} %x_ref.1), custom_call_target="tpu_custom_call" | custom-call | tf_op jit(solution)/shard_map/exchange/pallas_call | solution.py:404
  285.9 5.6 %finish.1 = (f32[16,24,8016]{2,1,0:T(8,128)}, f32[16,8016]{1,0:T(8,128)}, f32[16,24]{1,0:T(8,128)}, f32[1,16]{1,0:T(1,128)}) custom-call(f32[3,3,128]{2,1,0:T(4,128)S(1)} %get-tuple-element.10.tot_ref, f32[400,8064]{1,0:T(8,128)S(1)} %get-tuple-element.11.z_ref), custom_call_target="tpu_custom_call" | custom-call | tf_op jit(solution)/shard_map/finish/pallas_call | solution.py:435

commit v4 on v3

--- a/solution.py
+++ b/solution.py
@@ -49,11 +49,10 @@
         pl.when(jnp.logical_not(wide))(lambda: body(vp))
 
     core = lax.rem(my_b, 2)
+    inner = lax.rem(lax.div(my_a + 1, 2), 2)
 
     def nth(i):
-        r = lax.rem((n // 2 + 1) * i + n // 2, n)
-        far = lax.div(r, n // 2)
-        return far * (n // 2 + lax.rem(r + core * (n // 4), n // 2)) + (1 - far) * r
+        return inner * lax.rem((n // 2 + 1) * (i + core) + n // 2, n) + (1 - inner) * i
 
     def width_of(g):
         return vp if g < phases - 1 else vp - LANES
@@ -305,13 +304,12 @@
 
     for g in range(phases):
         def one(i, c, g=g):
-            r = nth(i)
-            a, b = peer(r)
+            a, b = peer(i)
             s = a * 4 + b
 
-            @pl.when(r > 0)
+            @pl.when(i > 0)
             def _():
-                q_copy(g, r, s).wait_recv()
+                q_copy(g, i, s).wait_recv()
             excess(g, s)
             return c
         lax.fori_loop(0, n, one, 0)

time: 292 us -> 291 us (level)
  no operation moved by 1% of the time
where the time goes in v4:
time: 291 us
  Pallas kernels  290 us (100%)
    pallas_call x1, Pallas kernels, local_step(): pl.pallas_call(functools.partial(exchange_kernel, n, phases, vl), name='e...  285 us

profile of v4, /device:TPU:0, one launch (start us, length us, event | category | flops | bytes accessed | tf_op | source)
XLA Modules:
  0.0 290.9 jit_solution(13351174940527433031)
XLA Ops:
  0.6 284.7 %exchange.1 = (f32[400,8064]{1,0:T(8,128)S(1)}, f32[3,3,128]{2,1,0:T(4,128)S(1)}) custom-call(bf16[400,3072]{1,0:T(8,128)(2,1)} %bitcast.8, bf16[8016,3072]{1,0:T(8,128)(2,1)} %bitcast.6, f32[24,128256]{1,0:T(8,128)} %bitcast.7, s32[16,24]{1,0:T(8,128)} %x_ref.1), custom_call_target="tpu_custom_call" | custom-call | tf_op jit(solution)/shard_map/exchange/pallas_call | solution.py:402
  285.3 5.6 %finish.1 = (f32[16,24,8016]{2,1,0:T(8,128)}, f32[16,8016]{1,0:T(8,128)}, f32[16,24]{1,0:T(8,128)}, f32[1,16]{1,0:T(1,128)}) custom-call(f32[3,3,128]{2,1,0:T(4,128)S(1)} %get-tuple-element.10.tot_ref, f32[400,8064]{1,0:T(8,128)S(1)} %get-tuple-element.11.z_ref), custom_call_target="tpu_custom_call" | custom-call | tf_op jit(solution)/shard_map/finish/pallas_call | solution.py:433

commit v5 on v4

--- a/solution.py
+++ b/solution.py
@@ -14,6 +14,7 @@
 ROWS = 8
 W_ROWS = 256
 W_BUFS = 4
+AHEAD = 4
 SCALE = 2.0 ** 64
 
 
@@ -26,7 +27,7 @@
 def exchange_kernel(n, phases, vl, hid_ref, w_ref, q_ref, x_ref, z_ref, tot_ref,
                     hid_v, hs, wbuf, sbuf, qbuf, x_v, colmax, colsum, scale, part, stat, zmsg,
                     in_sem, w_sem, ld_sem, qs_sem, qr_sem, ss_sem, sr_sem, zs_sem, zr_sem):
-    vp = z_ref.shape[1]
+    vp = qbuf.shape[3]
     tiles = vp // LANES
     last = vl - (tiles - 1) * LANES
     rows_all = z_ref.shape[0]
@@ -70,6 +71,9 @@
 
     def tile_of(j):
         return slice(j * LANES, (j + 1) * LANES)
+
+    def part_of(j):
+        return slice(j * LANES, min((j + 1) * LANES, vl))
 
     free = LANES - last
 
@@ -93,6 +97,11 @@
 
     def send_phase(g):
         def one(i, c):
+            if g < phases - 1:
+                @pl.when(i + AHEAD < n)
+                def _():
+                    start_load(g, i + AHEAD)
+
             @pl.when(i < n)
             def _():
                 r = nth(i)
@@ -131,33 +140,34 @@
 
     hid_copy = pltpu.make_async_copy(hid_ref, hid_v, in_sem.at[0])
     x_copy = pltpu.make_async_copy(x_ref, x_v, in_sem.at[1])
-    def start_load(g):
-        def one(i, c):
-            a, b = peer(nth(i))
-            k = a * 4 + b
-            sized(k, lambda width: load(g, k, width).start())
-            if g == 0:
-                sized(k, lambda width: load(phases - 1, k, width).start())
-            return c
-        lax.fori_loop(0, n, one, 0)
-    for g in range(phases - 1):
-        start_load(g)
+    barrier = pltpu.get_barrier_semaphore()
+
+    def greet(i, c):
+        a, b = peer(n - i)
+        pl.semaphore_signal(barrier, inc=1, device_id={"tpa": a, "tpb": b}, device_id_type=MESH)
+        return c
+    lax.fori_loop(1, n, greet, 0)
+
+    def start_load(g, i):
+        a, b = peer(nth(i))
+        k = a * 4 + b
+        for h in (0, phases - 1) if g == 0 else (g,):
+            sized(k, lambda width, h=h: load(h, k, width).start())
+
+    for i in range(AHEAD):
+        start_load(0, i)
+    x_copy.start()
+    pl.semaphore_wait(barrier, n - 1)
+
+    send_phase(0)
+    for g in range(1, phases - 1):
+        for i in range(AHEAD):
+            start_load(g, i)
     hid_copy.start()
-    x_copy.start()
     for c in range(W_BUFS):
         w_copy(c, c).start()
-
-    barrier = pltpu.get_barrier_semaphore()
-
-    def greet(r, c):
-        a, b = peer(r)
-        pl.semaphore_signal(barrier, inc=1, device_id={"tpa": a, "tpb": b}, device_id_type=MESH)
-        return c
-    lax.fori_loop(1, n, greet, 0)
-    pl.semaphore_wait(barrier, n - 1)
-
-    send_phase(0)
-    send_phase(1)
+    for g in range(1, phases - 1):
+        send_phase(g)
 
     hid_copy.wait()
     row = lax.broadcasted_iota(jnp.int32, (rows_all, rows_all), 0)
@@ -195,19 +205,22 @@
 
     def row_stats(t, carry):
         rows = pl.ds(pl.multiple_of(t * ROWS, ROWS), ROWS)
-        m = jnp.where(lane < last, z_ref[rows, tile_of(tiles - 1)], -jnp.inf)
+        ending = z_ref[rows, part_of(tiles - 1)]
+        m = z_ref[rows, part_of(0)]
+        for j in range(1, tiles - 1):
+            m = jnp.maximum(m, z_ref[rows, part_of(j)])
+        m = jnp.maximum(jnp.max(m, axis=1, keepdims=True), jnp.max(ending, axis=1, keepdims=True))
+        m = jnp.broadcast_to(m, (ROWS, LANES))
+        ending = jnp.exp(ending - m[:, 0:last])
+        z_ref[rows, part_of(tiles - 1)] = ending
+        s = jnp.zeros((ROWS, LANES), jnp.float32)
         for j in range(tiles - 1):
-            m = jnp.maximum(m, z_ref[rows, tile_of(j)])
-        m = jnp.broadcast_to(jnp.max(m, axis=1, keepdims=True), (ROWS, LANES))
-        s = jnp.zeros((ROWS, LANES), jnp.float32)
-        for j in range(tiles):
-            e = jnp.exp(z_ref[rows, tile_of(j)] - m)
-            if j == tiles - 1:
-                e = jnp.where(lane < last, e, 0.0)
-            z_ref[rows, tile_of(j)] = e
+            e = jnp.exp(z_ref[rows, part_of(j)] - m)
+            z_ref[rows, part_of(j)] = e
             s = s + e
+        s = jnp.sum(s, axis=1, keepdims=True) + jnp.sum(ending, axis=1, keepdims=True)
         colmax[rows, :] = m
-        colsum[rows, :] = jnp.broadcast_to(jnp.sum(s, axis=1, keepdims=True), (ROWS, LANES))
+        colsum[rows, :] = jnp.broadcast_to(s, (ROWS, LANES))
         return carry
     lax.fori_loop(0, rows_all // ROWS, row_stats, 0)
     spare = colmax.shape[0] - rows_all
@@ -251,7 +264,8 @@
     for t in range(draft_rows // ROWS, rows_all // ROWS):
         rows = slice(t * ROWS, (t + 1) * ROWS)
         for j in range(tiles):
-            z_ref[rows, tile_of(j)] = z_ref[rows, tile_of(j)] * scale[rows, :]
+            value = z_ref[rows, part_of(j)]
+            z_ref[rows, part_of(j)] = value * scale[rows, 0:value.shape[1]]
 
     x_copy.wait()
     lane_f = lane.astype(jnp.float32)
@@ -266,24 +280,32 @@
         token = jnp.broadcast_to(jnp.where(token < vl, token, -1.0), (ROWS, LANES))
         sc = scale[rows, :]
         z_sum = p_pick = q_pick = jnp.zeros((ROWS, LANES), jnp.float32)
-        for j in range(tiles):
-            if g == phases - 1 and j == tiles - 1:
-                q = jnp.where(lane < free, pltpu.roll(qbuf[0, s, :, tile_of(j)], free, 1),
-                              pltpu.roll(qbuf[1, s, :, tile_of(j)], (free - last) % LANES, 1))
-            else:
-                q = qbuf[g, s, :, tile_of(j)]
-            p = z_ref[rows, tile_of(j)] * sc
+        for j in range(tiles - 1):
+            q = qbuf[g, s, :, tile_of(j)]
+            p = z_ref[rows, part_of(j)] * sc
             d = jnp.maximum(p - q, 0.0)
-            if j == tiles - 1:
-                d = jnp.where(lane < last, d, 0.0)
-            z_ref[rows, tile_of(j)] = d
+            z_ref[rows, part_of(j)] = d
             z_sum = z_sum + d
             hit = lane_f == token - float(j * LANES)
             p_pick = jnp.where(hit, p, p_pick)
             q_pick = jnp.where(hit, q, q_pick)
+        j = tiles - 1
+        if g < phases - 1:
+            q = qbuf[g, s, :, tile_of(j)]
+        else:
+            q = jnp.where(lane < free, pltpu.roll(qbuf[0, s, :, tile_of(j)], free, 1),
+                          pltpu.roll(qbuf[1, s, :, tile_of(j)], (free - last) % LANES, 1))
+        q = q[:, 0:last]
+        p = z_ref[rows, part_of(j)] * sc[:, 0:last]
+        d = jnp.maximum(p - q, 0.0)
+        z_ref[rows, part_of(j)] = d
+        hit = (lane_f == token - float(j * LANES))[:, 0:last]
         part[0, rows, :] = z_sum
         part[1, rows, :] = p_pick
         part[2, rows, :] = q_pick
+        part[0, rows, 0:last] = z_sum[:, 0:last] + d
+        part[1, rows, 0:last] = jnp.where(hit, p, p_pick[:, 0:last])
+        part[2, rows, 0:last] = jnp.where(hit, q, q_pick[:, 0:last])
 
     def z_copy(g, r, s):
         a, b = peer(r)
@@ -316,8 +338,8 @@
         block = slice(g * n * ROWS, (g + 1) * n * ROWS)
         zmsg[g, me] = jnp.concatenate([jnp.sum(part[i, block, :].T, axis=0, keepdims=True) for i in range(3)], axis=0)
 
-        def send(r, c, g=g):
-            z_copy(g, r, me).start()
+        def send(i, c, g=g):
+            z_copy(g, n - i, me).start()
             return c
         lax.fori_loop(1, n, send, 0)
 
@@ -327,34 +349,58 @@
             z_copy(g, r, me).wait_send()
         stat_copy(r, me).wait_send()
         return c
+
+    def divide(g):
+        inverse = jnp.broadcast_to(1.0 / (tot_ref[g, 0:1, :] * SCALE), (n * ROWS, LANES)).T
+        scale[0:n * ROWS, :] = inverse
+
+        def one(s, c):
+            rows = pl.ds(pl.multiple_of(g * (n * ROWS) + s * ROWS, ROWS), ROWS)
+            inv = scale[pl.ds(pl.multiple_of(s * ROWS, ROWS), ROWS), :]
+            for j in range(tiles):
+                value = z_ref[rows, part_of(j)] * SCALE
+                z_ref[rows, part_of(j)] = value * inv[:, 0:value.shape[1]]
+            return c
+        lax.fori_loop(0, n, one, 0)
+
+    for g in range(phases - 1):
+        add_up(g)
+        divide(g)
     lax.fori_loop(1, n, drain, 0)
-    for g in range(phases):
-        add_up(g)
-
-
-def finish_kernel(n, phases, vl, tot_ref, z_ref, res_ref, bonus_ref, accept_ref, expected_ref, inverse, staged, staged_bonus, sem, bonus_sem):
+    add_up(phases - 1)
+
+
+def finish_kernel(n, phases, vl, tot_ref, z_ref, res_ref, bonus_ref, accept_ref, expected_ref, inverse, staged, sem, bonus_sem):
     width = n * ROWS
     num_draft = phases * ROWS
-    for g in range(phases):
-        inverse[g] = jnp.broadcast_to(1.0 / (tot_ref[g, 0:1, :] * SCALE), (width, LANES)).T
-
-    def block_copy(b):
-        return pltpu.make_async_copy(staged.at[b], res_ref.at[b], sem.at[b])
+    last = phases - 1
+
+    def ready_copy(g, b):
+        return pltpu.make_async_copy(z_ref.at[pl.ds(pl.multiple_of(g * width + b * ROWS, ROWS), ROWS), :],
+                                     res_ref.at[b, g * ROWS:(g + 1) * ROWS, :], sem.at[g, b])
+
+    def staged_copy(b):
+        return pltpu.make_async_copy(staged.at[b], res_ref.at[b, last * ROWS:, :], sem.at[last, b])
+
+    bonus_copy = pltpu.make_async_copy(z_ref.at[phases * width:phases * width + n, :], bonus_ref, bonus_sem)
+
+    def start(b, c):
+        for g in range(last):
+            ready_copy(g, b).start()
+        return c
+    lax.fori_loop(0, n, start, 0)
+    bonus_copy.start()
+    inverse[...] = jnp.broadcast_to(1.0 / (tot_ref[last, 0:1, :] * SCALE), (width, LANES)).T
 
     def one(b, c):
-        for g in range(phases):
-            inv = inverse[g, pl.ds(pl.multiple_of(b * ROWS, ROWS), ROWS), :]
-            rows = pl.ds(pl.multiple_of(g * width + b * ROWS, ROWS), ROWS)
-            for j in range(pl.cdiv(vl, LANES)):
-                w = min(LANES, vl - j * LANES)
-                value = (z_ref[rows, j * LANES:(j + 1) * LANES] * SCALE) * inv
-                staged[b, g * ROWS:(g + 1) * ROWS, j * LANES:j * LANES + w] = value[:, 0:w]
-        block_copy(b).start()
+        inv = inverse[pl.ds(pl.multiple_of(b * ROWS, ROWS), ROWS), :]
+        rows = pl.ds(pl.multiple_of(last * width + b * ROWS, ROWS), ROWS)
+        for j in range(pl.cdiv(vl, LANES)):
+            w = min(LANES, vl - j * LANES)
+            staged[b, :, j * LANES:j * LANES + w] = (z_ref[rows, j * LANES:j * LANES + w] * SCALE) * inv[:, 0:w]
+        staged_copy(b).start()
         return c
     lax.fori_loop(0, n, one, 0)
-    staged_bonus[...] = z_ref[phases * width:phases * width + n, 0:vl]
-    bonus_copy = pltpu.make_async_copy(staged_bonus, bonus_ref, bonus_sem)
-    bonus_copy.start()
 
     seq_of = lax.broadcasted_iota(jnp.int32, (n, width), 1) // ROWS == lax.broadcasted_iota(jnp.int32, (n, width), 0)
     pos_of = lax.broadcasted_iota(jnp.int32, (ROWS, width), 1) % ROWS == lax.broadcasted_iota(jnp.int32, (ROWS, width), 0)
@@ -379,7 +425,9 @@
     expected_ref[...] = total
 
     def finished(b, c):
-        block_copy(b).wait()
+        for g in range(last):
+            ready_copy(g, b).wait()
+        staged_copy(b).wait()
         return c
     lax.fori_loop(0, n, finished, 0)
     bonus_copy.wait()
@@ -402,7 +450,7 @@
         z, tot = pl.pallas_call(
             functools.partial(exchange_kernel, n, phases, vl),
             name="exchange",
-            out_shape=(pltpu.VMEM((rows, vp), f32), pltpu.VMEM((phases, 3, LANES), f32)),
+            out_shape=(pltpu.VMEM((rows, vl), f32), pltpu.VMEM((phases, 3, LANES), f32)),
             in_specs=[any_spec] * 4,
             out_specs=(vmem_spec, vmem_spec),
             scratch_shapes=[
@@ -437,8 +485,8 @@
                        jax.ShapeDtypeStruct((seqs, num_draft), f32), jax.ShapeDtypeStruct((1, seqs), f32)),
             in_specs=[vmem_spec, vmem_spec],
             out_specs=(any_spec, any_spec, vmem_spec, vmem_spec),
-            scratch_shapes=[pltpu.VMEM((phases, n * ROWS, LANES), f32), pltpu.VMEM((seqs, num_draft, vl), f32),
-                            pltpu.VMEM((seqs, vl), f32), pltpu.SemaphoreType.DMA((seqs,)), pltpu.SemaphoreType.DMA],
+            scratch_shapes=[pltpu.VMEM((n * ROWS, LANES), f32), pltpu.VMEM((seqs, ROWS, vl), f32),
+                            pltpu.SemaphoreType.DMA((phases, seqs)), pltpu.SemaphoreType.DMA],
             compiler_params=pltpu.CompilerParams(vmem_limit_bytes=32 * 2**20),
         )(tot, z)
         return accept, expected.reshape(seqs), residual, bonus

time: 291 us -> 290 us (level)
  no operation moved by 1% of the time
where the time goes in v5:
time: 290 us
  Pallas kernels  289 us (100%)
    pallas_call x1, Pallas kernels, local_step(): pl.pallas_call(functools.partial(exchange_kernel, n, phases, vl), name='e...  284 us

profile of v5, /device:TPU:0, one launch (start us, length us, event | category | flops | bytes accessed | tf_op | source)
XLA Modules:
  0.0 290.1 jit_solution(18420973427512699507)
XLA Ops:
  0.6 283.8 %exchange.1 = (f32[400,8016]{1,0:T(8,128)S(1)}, f32[3,3,128]{2,1,0:T(4,128)S(1)}) custom-call(bf16[400,3072]{1,0:T(8,128)(2,1)} %bitcast.8, bf16[8016,3072]{1,0:T(8,128)(2,1)} %bitcast.6, f32[24,128256]{1,0:T(8,128)} %bitcast.7, s32[16,24]{1,0:T(8,128)} %x_ref.1), custom_call_target="tpu_custom_call" | custom-call | tf_op jit(solution)/shard_map/exchange/pallas_call | solution.py:450
  284.4 5.7 %finish.1 = (f32[16,24,8016]{2,1,0:T(8,128)}, f32[16,8016]{1,0:T(8,128)}, f32[16,24]{1,0:T(8,128)}, f32[1,16]{1,0:T(1,128)}) custom-call(f32[3,3,128]{2,1,0:T(4,128)S(1)} %get-tuple-element.10.tot_ref, f32[400,8016]{1,0:T(8,128)S(1)} %get-tuple-element.11.z_ref), custom_call_target="tpu_custom_call" | custom-call | tf_op jit(solution)/shard_map/finish/pallas_call | solution.py:481

commit v6 on v5

--- a/solution.py
+++ b/solution.py
@@ -25,8 +25,8 @@
 
 
 def exchange_kernel(n, phases, vl, hid_ref, w_ref, q_ref, x_ref, z_ref, tot_ref,
-                    hid_v, hs, wbuf, sbuf, qbuf, x_v, colmax, colsum, scale, part, stat, zmsg,
-                    in_sem, w_sem, ld_sem, qs_sem, qr_sem, ss_sem, sr_sem, zs_sem, zr_sem):
+                    hid_v, hs, wbuf, sbuf, qbuf, x_v, colmax, colsum, scale, part, stat_core, stat_chip, stat_half, sum_core, sum_chip, sum_half, zmsg,
+                    in_sem, w_sem, ld_sem, qs_sem, qr_sem, swap_s, swap_r, chip_s, chip_r, zs_sem, zr_sem):
     vp = qbuf.shape[3]
     tiles = vp // LANES
     last = vl - (tiles - 1) * LANES
@@ -52,8 +52,15 @@
     core = lax.rem(my_b, 2)
     inner = lax.rem(lax.div(my_a + 1, 2), 2)
 
-    def nth(i):
-        return inner * lax.rem((n // 2 + 1) * (i + core) + n // 2, n) + (1 - inner) * i
+    def nth(g, i):
+        r = inner * lax.rem((n // 2 + 1) * (i + core) + n // 2, n) + (1 - inner) * i
+        if g == phases - 1:
+            far = lax.div(r, n // 2)
+            r = (1 - far) * r + far * (n // 2 + lax.rem(r + (1 - inner) * (n // 4), n // 2))
+        return r
+
+    def arrival_order(g, i):
+        return i
 
     def width_of(g):
         return vp if g < phases - 1 else vp - LANES
@@ -104,7 +111,7 @@
 
             @pl.when(i < n)
             def _():
-                r = nth(i)
+                r = nth(g, i)
                 a, b = peer(r)
                 k = a * 4 + b
                 if g == 0:
@@ -121,7 +128,7 @@
 
             @pl.when(i > 0)
             def _():
-                before = nth(i - 1)
+                before = nth(g, i - 1)
 
                 @pl.when(before > 0)
                 def _():
@@ -149,7 +156,7 @@
     lax.fori_loop(1, n, greet, 0)
 
     def start_load(g, i):
-        a, b = peer(nth(i))
+        a, b = peer(nth(g, i))
         k = a * 4 + b
         for h in (0, phases - 1) if g == 0 else (g,):
             sized(k, lambda width, h=h: load(h, k, width).start())
@@ -223,6 +230,43 @@
         colsum[rows, :] = jnp.broadcast_to(s, (ROWS, LANES))
         return carry
     lax.fori_loop(0, rows_all // ROWS, row_stats, 0)
+    chip = my_a * 2 + lax.div(my_b, 2)
+    chips = n // 2
+
+    def swap(i, ref):
+        return pltpu.make_async_remote_copy(
+            src_ref=ref.at[core], dst_ref=ref.at[core], send_sem=swap_s.at[i], recv_sem=swap_r.at[i],
+            device_id={"tpa": my_a, "tpb": my_b + 1 - 2 * core}, device_id_type=MESH)
+
+    def swap_arrival(i, ref):
+        return pltpu.make_async_remote_copy(
+            src_ref=ref.at[1 - core], dst_ref=ref.at[1 - core], send_sem=swap_s.at[i], recv_sem=swap_r.at[i],
+            device_id={"tpa": my_a, "tpb": my_b}, device_id_type=MESH)
+
+    def chip_copy(i, ref, h, slot):
+        a, b = peer(2 * h)
+        return pltpu.make_async_remote_copy(
+            src_ref=ref.at[chip], dst_ref=ref.at[slot], send_sem=chip_s.at[i, h], recv_sem=chip_r.at[i, slot],
+            device_id={"tpa": a, "tpb": b}, device_id_type=MESH)
+
+    def chip_send(i, ref):
+        for h in range(chips - 1, 0, -1):
+            chip_copy(i, ref, h, chip).start()
+
+    def chip_arrivals(i, ref):
+        for h in range(1, chips):
+            a, b = peer(2 * h)
+            chip_copy(i, ref, h, a * 2 + lax.div(b, 2)).wait_recv()
+
+    def combine(pairs):
+        top = pairs[0][0]
+        for m, _ in pairs[1:]:
+            top = jnp.maximum(top, m)
+        total = jnp.zeros_like(top)
+        for m, s in pairs:
+            total = total + s * jnp.exp(m - top)
+        return top, total
+
     spare = colmax.shape[0] - rows_all
     colmax[rows_all:, :] = jnp.zeros((spare, LANES), jnp.float32)
     colsum[rows_all:, :] = jnp.ones((spare, LANES), jnp.float32)
@@ -231,33 +275,28 @@
 
     def as_rows(ref):
         return jnp.concatenate([ref[i * LANES:(i + 1) * LANES, :].T[0:1, :] for i in range(blocks)], axis=0)
-    stat[me, 0] = as_rows(colmax)
-    stat[me, 1] = as_rows(colsum)
-
-    def stat_copy(r, s):
-        a, b = peer(r)
-        return pltpu.make_async_remote_copy(
-            src_ref=stat.at[me], dst_ref=stat.at[s], send_sem=ss_sem.at[r], recv_sem=sr_sem.at[s],
-            device_id={"tpa": a, "tpb": b}, device_id_type=MESH)
-
-    def send_stat(r, c):
-        stat_copy(r, me).start()
-        return c
-    lax.fori_loop(1, n, send_stat, 0)
+    my_max = as_rows(colmax)
+    stat_core[core, 0] = my_max
+    stat_core[core, 1] = as_rows(colsum)
+    swap(0, stat_core).start()
+    swap_arrival(0, stat_core).wait_recv()
+    top, total = combine([(stat_core[c, 0], stat_core[c, 1]) for c in range(2)])
+    half = blocks // 2
+    mine = core == 0
+    stat_chip[chip, 0] = jnp.where(mine, top[0:half], top[half:])
+    stat_chip[chip, 1] = jnp.where(mine, total[0:half], total[half:])
+    chip_send(0, stat_chip)
     send_phase(2)
 
-    def wait_stat(r, c):
-        a, b = peer(r)
-        stat_copy(r, a * 4 + b).wait_recv()
-        return c
-    lax.fori_loop(1, n, wait_stat, 0)
-    glob_max = stat[0, 0]
-    for s in range(1, n):
-        glob_max = jnp.maximum(glob_max, stat[s, 0])
-    glob_sum = jnp.zeros_like(glob_max)
-    for s in range(n):
-        glob_sum = glob_sum + stat[s, 1] * jnp.exp(stat[s, 0] - glob_max)
-    factor = jnp.exp(stat[me, 0] - glob_max) / glob_sum
+    chip_arrivals(0, stat_chip)
+    top, total = combine([(stat_chip[c, 0], stat_chip[c, 1]) for c in range(chips)])
+    stat_half[core, 0] = top
+    stat_half[core, 1] = total
+    swap(1, stat_half).start()
+    swap_arrival(1, stat_half).wait_recv()
+    top = jnp.concatenate([stat_half[0, 0], stat_half[1, 0]], axis=0)
+    total = jnp.concatenate([stat_half[0, 1], stat_half[1, 1]], axis=0)
+    factor = jnp.exp(stat_core[core, 0] - top) / total
     for i in range(blocks):
         scale[i * LANES:(i + 1) * LANES, :] = jnp.broadcast_to(factor[i:i + 1, :], (LANES, LANES)).T
 
@@ -307,47 +346,43 @@
         part[1, rows, 0:last] = jnp.where(hit, p, p_pick[:, 0:last])
         part[2, rows, 0:last] = jnp.where(hit, q, q_pick[:, 0:last])
 
-    def z_copy(g, r, s):
+    def z_copy(r, s):
         a, b = peer(r)
         return pltpu.make_async_remote_copy(
-            src_ref=zmsg.at[g, me], dst_ref=zmsg.at[g, s], send_sem=zs_sem.at[g, r], recv_sem=zr_sem.at[g, s],
+            src_ref=zmsg.at[me], dst_ref=zmsg.at[s], send_sem=zs_sem.at[r], recv_sem=zr_sem.at[s],
             device_id={"tpa": a, "tpb": b}, device_id_type=MESH)
 
-    def add_up(g):
-        def arrived(r, c):
-            a, b = peer(r)
-            z_copy(g, r, a * 4 + b).wait_recv()
-            return c
-        lax.fori_loop(1, n, arrived, 0)
-        total = zmsg[g, 0]
-        for s in range(1, n):
-            total = total + zmsg[g, s]
-        tot_ref[g] = total
+    def row_sums(g):
+        block = slice(g * n * ROWS, (g + 1) * n * ROWS)
+        return jnp.concatenate([jnp.sum(part[i, block, :].T, axis=0, keepdims=True) for i in range(3)], axis=0)
 
     for g in range(phases):
         def one(i, c, g=g):
-            a, b = peer(i)
+            r = arrival_order(g, i)
+            a, b = peer(r)
             s = a * 4 + b
 
-            @pl.when(i > 0)
+            @pl.when(r > 0)
             def _():
-                q_copy(g, i, s).wait_recv()
+                q_copy(g, r, s).wait_recv()
             excess(g, s)
             return c
         lax.fori_loop(0, n, one, 0)
-        block = slice(g * n * ROWS, (g + 1) * n * ROWS)
-        zmsg[g, me] = jnp.concatenate([jnp.sum(part[i, block, :].T, axis=0, keepdims=True) for i in range(3)], axis=0)
-
-        def send(i, c, g=g):
-            z_copy(g, n - i, me).start()
-            return c
-        lax.fori_loop(1, n, send, 0)
+        if g == phases - 2:
+            for h in range(2):
+                sum_core[core, h] = row_sums(h)
+            swap(2, sum_core).start()
+            swap_arrival(2, sum_core).wait_recv()
+            sum_chip[chip] = jnp.where(mine, sum_core[0, 0] + sum_core[1, 0], sum_core[0, 1] + sum_core[1, 1])
+            chip_send(1, sum_chip)
+    zmsg[me] = row_sums(phases - 1)
+    for r in range(n - 1, 0, -1):
+        z_copy(r, me).start()
 
     def drain(r, c):
         for g in range(phases):
             q_copy(g, r, me).wait_send()
-            z_copy(g, r, me).wait_send()
-        stat_copy(r, me).wait_send()
+        z_copy(r, me).wait_send()
         return c
 
     def divide(g):
@@ -363,11 +398,29 @@
             return c
         lax.fori_loop(0, n, one, 0)
 
+    chip_arrivals(1, sum_chip)
+    total = sum_chip[0]
+    for c in range(1, chips):
+        total = total + sum_chip[c]
+    sum_half[core] = total
+    swap(3, sum_half).start()
+    swap_arrival(3, sum_half).wait_recv()
     for g in range(phases - 1):
-        add_up(g)
+        tot_ref[g] = sum_half[g]
         divide(g)
     lax.fori_loop(1, n, drain, 0)
-    add_up(phases - 1)
+    for i, ref in enumerate((stat_core, stat_half, sum_core, sum_half)):
+        swap(i, ref).wait_send()
+    for i, ref in enumerate((stat_chip, sum_chip)):
+        for h in range(1, chips):
+            chip_copy(i, ref, h, chip).wait_send()
+    for r in range(1, n):
+        a, b = peer(r)
+        z_copy(r, a * 4 + b).wait_recv()
+    total = zmsg[0]
+    for s in range(1, n):
+        total = total + zmsg[s]
+    tot_ref[phases - 1] = total
 
 
 def finish_kernel(n, phases, vl, tot_ref, z_ref, res_ref, bonus_ref, accept_ref, expected_ref, inverse, staged, sem, bonus_sem):
@@ -386,7 +439,7 @@
 
     def start(b, c):
         for g in range(last):
-            ready_copy(g, b).start()
+            ready_copy(g, b).start(priority=g % 2)
         return c
     lax.fori_loop(0, n, start, 0)
     bonus_copy.start()
@@ -464,17 +517,24 @@
                 pltpu.VMEM((stat_rows, LANES), f32),
                 pltpu.VMEM((stat_rows, LANES), f32),
                 pltpu.VMEM((3, phases * n * ROWS, LANES), f32),
-                pltpu.VMEM((n, 2, stat_rows // LANES, LANES), f32),
-                pltpu.VMEM((phases, n, 3, LANES), f32),
+                pltpu.VMEM((2, 2, stat_rows // LANES, LANES), f32),
+                pltpu.VMEM((n // 2, 2, stat_rows // LANES // 2, LANES), f32),
+                pltpu.VMEM((2, 2, stat_rows // LANES // 2, LANES), f32),
+                pltpu.VMEM((2, 2, 3, LANES), f32),
+                pltpu.VMEM((n // 2, 3, LANES), f32),
+                pltpu.VMEM((2, 3, LANES), f32),
+                pltpu.VMEM((n, 3, LANES), f32),
                 pltpu.SemaphoreType.DMA((2,)),
                 pltpu.SemaphoreType.DMA((W_BUFS,)),
                 pltpu.SemaphoreType.DMA((phases, n)),
                 pltpu.SemaphoreType.DMA((phases, n)),
                 pltpu.SemaphoreType.DMA((phases, n)),
+                pltpu.SemaphoreType.DMA((4,)),
+                pltpu.SemaphoreType.DMA((4,)),
+                pltpu.SemaphoreType.DMA((2, n // 2)),
+                pltpu.SemaphoreType.DMA((2, n // 2)),
                 pltpu.SemaphoreType.DMA((n,)),
                 pltpu.SemaphoreType.DMA((n,)),
-                pltpu.SemaphoreType.DMA((phases, n)),
-                pltpu.SemaphoreType.DMA((phases, n)),
             ],
             compiler_params=pltpu.CompilerParams(collective_id=0, has_side_effects=True, vmem_limit_bytes=48 * 2**20),
         )(hidden.transpose(1, 0, 2).reshape(rows, depth), w_head.T, q_draft.reshape(num_draft, q_draft.shape[2]), x_draft)

time: 290 us -> 287 us (0.990)
  Pallas kernels: 289 us -> 286 us
    pallas_call x1, Pallas kernels: 284 us -> 281 us  [local_step(): pl.pallas_call(functools.partial(exchange_kernel, n, phases, vl), name='e...]
where the time goes in v6:
time: 287 us
  Pallas kernels  286 us (100%)
    pallas_call x1, Pallas kernels, local_step(): pl.pallas_call(functools.partial(exchange_kernel, n, phases, vl), name='e...  281 us

profile of v6, /device:TPU:0, one launch (start us, length us, event | category | flops | bytes accessed | tf_op | source)
XLA Modules:
  0.0 286.9 jit_solution(4409430271937993689)
XLA Ops:
  0.6 280.6 %exchange.1 = (f32[400,8016]{1,0:T(8,128)S(1)}, f32[3,3,128]{2,1,0:T(4,128)S(1)}) custom-call(bf16[400,3072]{1,0:T(8,128)(2,1)} %bitcast.8, bf16[8016,3072]{1,0:T(8,128)(2,1)} %bitcast.6, f32[24,128256]{1,0:T(8,128)} %bitcast.7, s32[16,24]{1,0:T(8,128)} %x_ref.1), custom_call_target="tpu_custom_call" | custom-call | tf_op jit(solution)/shard_map/exchange/pallas_call | solution.py:503
  281.2 5.7 %finish.1 = (f32[16,24,8016]{2,1,0:T(8,128)}, f32[16,8016]{1,0:T(8,128)}, f32[16,24]{1,0:T(8,128)}, f32[1,16]{1,0:T(1,128)}) custom-call(f32[3,3,128]{2,1,0:T(4,128)S(1)} %get-tuple-element.10.tot_ref, f32[400,8016]{1,0:T(8,128)S(1)} %get-tuple-element.11.z_ref), custom_call_target="tpu_custom_call" | custom-call | tf_op jit(solution)/shard_map/finish/pallas_call | solution.py:541

commit v7 on v6

--- a/solution.py
+++ b/solution.py
@@ -36,7 +36,12 @@
     me = my_a * 4 + my_b
     lane = lax.broadcasted_iota(jnp.int32, (ROWS, LANES), 1)
 
+    def flip(a, r):
+        return (a, a + 1 - 2 * lax.rem(a, 2), lax.rem(a + 2, 4), 3 - a)[r]
+
     def peer(r):
+        if isinstance(r, int):
+            return flip(my_a, r // 4), flip(my_b, r % 4)
         return xor4(my_a, lax.div(r, 4)), xor4(my_b, lax.rem(r, 4))
 
     def window(k):
@@ -60,7 +65,8 @@
         return r
 
     def arrival_order(g, i):
-        return i
+        far = lax.div(i, n // 2)
+        return i if g < phases - 1 else (1 - far) * i + far * (n // 2 + lax.rem(i + n // 4, n // 2))
 
     def width_of(g):
         return vp if g < phases - 1 else vp - LANES
@@ -102,39 +108,42 @@
             this = following
         sbuf[g, k, :, tile_of(tiles - 1)] = ending
 
+    def ready(g, i):
+        if g < phases - 1:
+            @pl.when(i + AHEAD < n)
+            def _():
+                start_load(g, i + AHEAD)
+        r = nth(g, i)
+        a, b = peer(r)
+        k = a * 4 + b
+        if g == 0:
+            sized(k, lambda width: load(0, k, width).wait())
+            sized(k, lambda width: load(phases - 1, k, width).wait())
+        elif g < phases - 1:
+            sized(k, lambda width: load(g, k, width).wait())
+        prepare(g, k)
+
+        @pl.when(r == 0)
+        def _():
+            for j in range(tiles):
+                qbuf[g, me, :, tile_of(j)] = sbuf[g, me, :, tile_of(j)]
+
+    def first(g):
+        lax.fori_loop(0, 2, lambda i, c: (ready(g, i), c)[1], 0)
+
     def send_phase(g):
         def one(i, c):
-            if g < phases - 1:
-                @pl.when(i + AHEAD < n)
-                def _():
-                    start_load(g, i + AHEAD)
-
-            @pl.when(i < n)
+            r = nth(g, i)
+
+            @pl.when(r > 0)
             def _():
-                r = nth(g, i)
-                a, b = peer(r)
-                k = a * 4 + b
-                if g == 0:
-                    sized(k, lambda width: load(0, k, width).wait())
-                    sized(k, lambda width: load(phases - 1, k, width).wait())
-                elif g < phases - 1:
-                    sized(k, lambda width: load(g, k, width).wait())
-                prepare(g, k)
-
-                @pl.when(r == 0)
-                def _():
-                    for j in range(tiles):
-                        qbuf[g, me, :, tile_of(j)] = sbuf[g, me, :, tile_of(j)]
-
-            @pl.when(i > 0)
+                q_copy(g, r, me).start()
+
+            @pl.when(i + 2 < n)
             def _():
-                before = nth(g, i - 1)
-
-                @pl.when(before > 0)
-                def _():
-                    q_copy(g, before, me).start()
+                ready(g, i + 2)
             return c
-        lax.fori_loop(0, n + 1, one, 0)
+        lax.fori_loop(0, n, one, 0)
 
     def w_copy(c, slot):
         return pltpu.make_async_copy(w_ref.at[pl.ds(pl.multiple_of(c * W_ROWS, W_ROWS), W_ROWS), :], wbuf.at[slot], w_sem.at[slot])
@@ -149,11 +158,9 @@
     x_copy = pltpu.make_async_copy(x_ref, x_v, in_sem.at[1])
     barrier = pltpu.get_barrier_semaphore()
 
-    def greet(i, c):
-        a, b = peer(n - i)
+    for r in range(n - 1, 0, -1):
+        a, b = peer(r)
         pl.semaphore_signal(barrier, inc=1, device_id={"tpa": a, "tpb": b}, device_id_type=MESH)
-        return c
-    lax.fori_loop(1, n, greet, 0)
 
     def start_load(g, i):
         a, b = peer(nth(g, i))
@@ -164,6 +171,7 @@
     for i in range(AHEAD):
         start_load(0, i)
     x_copy.start()
+    first(0)
     pl.semaphore_wait(barrier, n - 1)
 
     send_phase(0)
@@ -174,6 +182,7 @@
     for c in range(W_BUFS):
         w_copy(c, c).start()
     for g in range(1, phases - 1):
+        first(g)
         send_phase(g)
 
     hid_copy.wait()
@@ -286,7 +295,8 @@
     stat_chip[chip, 0] = jnp.where(mine, top[0:half], top[half:])
     stat_chip[chip, 1] = jnp.where(mine, total[0:half], total[half:])
     chip_send(0, stat_chip)
-    send_phase(2)
+    first(phases - 1)
+    send_phase(phases - 1)
 
     chip_arrivals(0, stat_chip)
     top, total = combine([(stat_chip[c, 0], stat_chip[c, 1]) for c in range(chips)])
@@ -339,12 +349,9 @@
         d = jnp.maximum(p - q, 0.0)
         z_ref[rows, part_of(j)] = d
         hit = (lane_f == token - float(j * LANES))[:, 0:last]
-        part[0, rows, :] = z_sum
-        part[1, rows, :] = p_pick
-        part[2, rows, :] = q_pick
-        part[0, rows, 0:last] = z_sum[:, 0:last] + d
-        part[1, rows, 0:last] = jnp.where(hit, p, p_pick[:, 0:last])
-        part[2, rows, 0:last] = jnp.where(hit, q, q_pick[:, 0:last])
+        sums = [jnp.sum(whole, axis=1, keepdims=True) + jnp.sum(ending, axis=1, keepdims=True)
+                for whole, ending in ((z_sum, d), (p_pick, jnp.where(hit, p, 0.0)), (q_pick, jnp.where(hit, q, 0.0)))]
+        part[rows, :] = jnp.where(lane == 0, sums[0], jnp.where(lane == 1, sums[1], sums[2]))
 
     def z_copy(r, s):
         a, b = peer(r)
@@ -354,7 +361,7 @@
 
     def row_sums(g):
         block = slice(g * n * ROWS, (g + 1) * n * ROWS)
-        return jnp.concatenate([jnp.sum(part[i, block, :].T, axis=0, keepdims=True) for i in range(3)], axis=0)
+        return part[block, :].T[0:3, :]
 
     for g in range(phases):
         def one(i, c, g=g):
@@ -516,7 +523,7 @@
                 pltpu.VMEM((stat_rows, LANES), f32),
                 pltpu.VMEM((stat_rows, LANES), f32),
                 pltpu.VMEM((stat_rows, LANES), f32),
-                pltpu.VMEM((3, phases * n * ROWS, LANES), f32),
+                pltpu.VMEM((phases * n * ROWS, LANES), f32),
                 pltpu.VMEM((2, 2, stat_rows // LANES, LANES), f32),
                 pltpu.VMEM((n // 2, 2, stat_rows // LANES // 2, LANES), f32),
                 pltpu.VMEM((2, 2, stat_rows // LANES // 2, LANES), f32),

time: 287 us -> 287 us (level)
  no operation moved by 1% of the time
where the time goes in v7:
time: 287 us
  Pallas kernels  286 us (100%)
    pallas_call x1, Pallas kernels, local_step(): pl.pallas_call(functools.partial(exchange_kernel, n, phases, vl), name='e...  281 us

profile of v7, /device:TPU:0, one launch (start us, length us, event | category | flops | bytes accessed | tf_op | source)
XLA Modules:
  0.0 287.0 jit_solution(13555749060800497786)
XLA Ops:
  0.6 280.7 %exchange.1 = (f32[400,8016]{1,0:T(8,128)S(1)}, f32[3,3,128]{2,1,0:T(4,128)S(1)}) custom-call(bf16[400,3072]{1,0:T(8,128)(2,1)} %bitcast.8, bf16[8016,3072]{1,0:T(8,128)(2,1)} %bitcast.6, f32[24,128256]{1,0:T(8,128)} %bitcast.7, s32[16,24]{1,0:T(8,128)} %x_ref.1), custom_call_target="tpu_custom_call" | custom-call | tf_op jit(solution)/shard_map/exchange/pallas_call | solution.py:510
  281.3 5.7 %finish.1 = (f32[16,24,8016]{2,1,0:T(8,128)}, f32[16,8016]{1,0:T(8,128)}, f32[16,24]{1,0:T(8,128)}, f32[1,16]{1,0:T(1,128)}) custom-call(f32[3,3,128]{2,1,0:T(4,128)S(1)} %get-tuple-element.10.tot_ref, f32[400,8016]{1,0:T(8,128)S(1)} %get-tuple-element.11.z_ref), custom_call_target="tpu_custom_call" | custom-call | tf_op jit(solution)/shard_map/finish/pallas_call | solution.py:548

commit v8 on v7

--- a/solution.py
+++ b/solution.py
@@ -58,11 +58,13 @@
     inner = lax.rem(lax.div(my_a + 1, 2), 2)
 
     def nth(g, i):
-        r = inner * lax.rem((n // 2 + 1) * (i + core) + n // 2, n) + (1 - inner) * i
-        if g == phases - 1:
-            far = lax.div(r, n // 2)
-            r = (1 - far) * r + far * (n // 2 + lax.rem(r + (1 - inner) * (n // 4), n // 2))
-        return r
+        if g < phases - 1:
+            return inner * lax.rem((n // 2 + 1) * (i + core) + n // 2, n) + (1 - inner) * i
+        j = lax.div(i, 2)
+        is_far = lax.rem(i + core + 1, 2)
+        by_turns = is_far * jnp.where(j < n // 4, 3 * n // 4 - 1 - j, n + n // 4 - 1 - j) + (1 - is_far) * j
+        in_turn = jnp.where(i < n // 2, i, n + n // 2 - 1 - i)
+        return inner * by_turns + (1 - inner) * in_turn
 
     def arrival_order(g, i):
         far = lax.div(i, n // 2)
@@ -430,7 +432,7 @@
     tot_ref[phases - 1] = total
 
 
-def finish_kernel(n, phases, vl, tot_ref, z_ref, res_ref, bonus_ref, accept_ref, expected_ref, inverse, staged, sem, bonus_sem):
+def finish_kernel(n, phases, vl, tot_ref, z_ref, res_ref, bonus_ref, accept_ref, expected_ref, inverse, staged, accepted, expected, sem, bonus_sem, small_sem):
     width = n * ROWS
     num_draft = phases * ROWS
     last = phases - 1
@@ -476,13 +478,17 @@
                                   precision=lax.Precision.HIGHEST, preferred_element_type=jnp.float32)
         by_pos.append(jnp.dot(jnp.where(pos_of, jnp.broadcast_to(a, (ROWS, width)), 0.0), to_seq,
                               precision=lax.Precision.HIGHEST, preferred_element_type=jnp.float32))
-    accept_ref[...] = by_seq
+    accepted[...] = by_seq
+    accept_copy = pltpu.make_async_copy(accepted, accept_ref, small_sem.at[0])
+    accept_copy.start()
     product = by_pos[0][0:1, :]
     total = product
     for k in range(1, num_draft):
         product = product * by_pos[k // ROWS][k % ROWS:k % ROWS + 1, :]
         total = total + product
-    expected_ref[...] = total
+    expected[...] = total
+    expected_copy = pltpu.make_async_copy(expected, expected_ref, small_sem.at[1])
+    expected_copy.start()
 
     def finished(b, c):
         for g in range(last):
@@ -491,6 +497,8 @@
         return c
     lax.fori_loop(0, n, finished, 0)
     bonus_copy.wait()
+    accept_copy.wait()
+    expected_copy.wait()
 
 
 def solution(mesh):
@@ -551,9 +559,10 @@
             out_shape=(jax.ShapeDtypeStruct((seqs, num_draft, vl), f32), jax.ShapeDtypeStruct((seqs, vl), f32),
                        jax.ShapeDtypeStruct((seqs, num_draft), f32), jax.ShapeDtypeStruct((1, seqs), f32)),
             in_specs=[vmem_spec, vmem_spec],
-            out_specs=(any_spec, any_spec, vmem_spec, vmem_spec),
+            out_specs=(any_spec,) * 4,
             scratch_shapes=[pltpu.VMEM((n * ROWS, LANES), f32), pltpu.VMEM((seqs, ROWS, vl), f32),
-                            pltpu.SemaphoreType.DMA((phases, seqs)), pltpu.SemaphoreType.DMA],
+                            pltpu.VMEM((seqs, num_draft), f32), pltpu.VMEM((1, seqs), f32),
+                            pltpu.SemaphoreType.DMA((phases, seqs)), pltpu.SemaphoreType.DMA, pltpu.SemaphoreType.DMA((2,))],
             compiler_params=pltpu.CompilerParams(vmem_limit_bytes=32 * 2**20),
         )(tot, z)
         return accept, expected.reshape(seqs), residual, bonus

time: 287 us -> 287 us (level)
  no operation moved by 1% of the time
where the time goes in v8:
time: 287 us
  Pallas kernels  286 us (100%)
    pallas_call x1, Pallas kernels, local_step(): pl.pallas_call(functools.partial(exchange_kernel, n, phases, vl), name='e...  281 us

profile of v8, /device:TPU:0, one launch (start us, length us, event | category | flops | bytes accessed | tf_op | source)
XLA Modules:
  0.0 287.0 jit_solution(10172047841437646217)
XLA Ops:
  0.6 281.3 %exchange.1 = (f32[400,8016]{1,0:T(8,128)S(1)}, f32[3,3,128]{2,1,0:T(4,128)S(1)}) custom-call(bf16[400,3072]{1,0:T(8,128)(2,1)} %bitcast.8, bf16[8016,3072]{1,0:T(8,128)(2,1)} %bitcast.6, f32[24,128256]{1,0:T(8,128)} %bitcast.7, s32[16,24]{1,0:T(8,128)} %x_ref.1), custom_call_target="tpu_custom_call" | custom-call | tf_op jit(solution)/shard_map/exchange/pallas_call | solution.py:518
  281.9 5.1 %finish.1 = (f32[16,24,8016]{2,1,0:T(8,128)}, f32[16,8016]{1,0:T(8,128)}, f32[16,24]{1,0:T(8,128)}, f32[1,16]{1,0:T(1,128)}) custom-call(f32[3,3,128]{2,1,0:T(4,128)S(1)} %get-tuple-element.10.tot_ref, f32[400,8016]{1,0:T(8,128)S(1)} %get-tuple-element.11.z_ref), custom_call_target="tpu_custom_call" | custom-call | tf_op jit(solution)/shard_map/finish/pallas_call | solution.py:556

commit v9 on v8

--- a/solution.py
+++ b/solution.py
@@ -57,18 +57,17 @@
     core = lax.rem(my_b, 2)
     inner = lax.rem(lax.div(my_a + 1, 2), 2)
 
-    def nth(g, i):
-        if g < phases - 1:
-            return inner * lax.rem((n // 2 + 1) * (i + core) + n // 2, n) + (1 - inner) * i
+    def far_peer(f):
+        return n // 2 + n // 4 * lax.rem(f + core, 2) + lax.div(f, 2)
+
+    def nth(i):
         j = lax.div(i, 2)
-        is_far = lax.rem(i + core + 1, 2)
-        by_turns = is_far * jnp.where(j < n // 4, 3 * n // 4 - 1 - j, n + n // 4 - 1 - j) + (1 - is_far) * j
-        in_turn = jnp.where(i < n // 2, i, n + n // 2 - 1 - i)
-        return inner * by_turns + (1 - inner) * in_turn
-
-    def arrival_order(g, i):
-        far = lax.div(i, n // 2)
-        return i if g < phases - 1 else (1 - far) * i + far * (n // 2 + lax.rem(i + n // 4, n // 2))
+        by_turns = jnp.where(lax.rem(i + core, 2) == 0, far_peer(j), j)
+        in_turn = jnp.where(i < n // 2, i, far_peer(lax.rem(i, n // 2)))
+        return jnp.where(inner == 1, by_turns, in_turn)
+
+    def arrival_order(i):
+        return jnp.where(i < n // 2, i, far_peer(lax.rem(i, n // 2)))
 
     def width_of(g):
         return vp if g < phases - 1 else vp - LANES
@@ -115,7 +114,7 @@
             @pl.when(i + AHEAD < n)
             def _():
                 start_load(g, i + AHEAD)
-        r = nth(g, i)
+        r = nth(i)
         a, b = peer(r)
         k = a * 4 + b
         if g == 0:
@@ -135,7 +134,7 @@
 
     def send_phase(g):
         def one(i, c):
-            r = nth(g, i)
+            r = nth(i)
 
             @pl.when(r > 0)
             def _():
@@ -165,7 +164,7 @@
         pl.semaphore_signal(barrier, inc=1, device_id={"tpa": a, "tpb": b}, device_id_type=MESH)
 
     def start_load(g, i):
-        a, b = peer(nth(g, i))
+        a, b = peer(nth(i))
         k = a * 4 + b
         for h in (0, phases - 1) if g == 0 else (g,):
             sized(k, lambda width, h=h: load(h, k, width).start())
@@ -367,7 +366,7 @@
 
     for g in range(phases):
         def one(i, c, g=g):
-            r = arrival_order(g, i)
+            r = arrival_order(i)
             a, b = peer(r)
             s = a * 4 + b
 

time: 287 us -> 288 us (level)
  no operation moved by 1% of the time
where the time goes in v9:
time: 288 us
  Pallas kernels  287 us (100%)
    pallas_call x1, Pallas kernels, local_step(): pl.pallas_call(functools.partial(exchange_kernel, n, phases, vl), name='e...  282 us

profile of v9, /device:TPU:0, one launch (start us, length us, event | category | flops | bytes accessed | tf_op | source)
XLA Modules:
  0.0 288.0 jit_solution(3990241601506462638)
XLA Ops:
  0.6 282.3 %exchange.1 = (f32[400,8016]{1,0:T(8,128)S(1)}, f32[3,3,128]{2,1,0:T(4,128)S(1)}) custom-call(bf16[400,3072]{1,0:T(8,128)(2,1)} %bitcast.8, bf16[8016,3072]{1,0:T(8,128)(2,1)} %bitcast.6, f32[24,128256]{1,0:T(8,128)} %bitcast.7, s32[16,24]{1,0:T(8,128)} %x_ref.1), custom_call_target="tpu_custom_call" | custom-call | tf_op jit(solution)/shard_map/exchange/pallas_call | solution.py:517
  282.9 5.1 %finish.1 = (f32[16,24,8016]{2,1,0:T(8,128)}, f32[16,8016]{1,0:T(8,128)}, f32[16,24]{1,0:T(8,128)}, f32[1,16]{1,0:T(1,128)}) custom-call(f32[3,3,128]{2,1,0:T(4,128)S(1)} %get-tuple-element.10.tot_ref, f32[400,8016]{1,0:T(8,128)S(1)} %get-tuple-element.11.z_ref), custom_call_target="tpu_custom_call" | custom-call | tf_op jit(solution)/shard_map/finish/pallas_call | solution.py:555

commit v10 on v8

--- a/solution.py
+++ b/solution.py
@@ -57,31 +57,30 @@
     core = lax.rem(my_b, 2)
     inner = lax.rem(lax.div(my_a + 1, 2), 2)
 
-    def nth(g, i):
-        if g < phases - 1:
-            return inner * lax.rem((n // 2 + 1) * (i + core) + n // 2, n) + (1 - inner) * i
-        j = lax.div(i, 2)
-        is_far = lax.rem(i + core + 1, 2)
-        by_turns = is_far * jnp.where(j < n // 4, 3 * n // 4 - 1 - j, n + n // 4 - 1 - j) + (1 - is_far) * j
-        in_turn = jnp.where(i < n // 2, i, n + n // 2 - 1 - i)
-        return inner * by_turns + (1 - inner) * in_turn
+    def nth(stage, i):
+        r = inner * lax.rem((n // 2 + 1) * (i + core) + n // 2, n) + (1 - inner) * i
+        if stage == 1:
+            far = lax.div(r, n // 2)
+            r = (1 - far) * r + far * (n // 2 + lax.rem(r + (1 - inner) * (n // 4), n // 2))
+        return r
 
     def arrival_order(g, i):
         far = lax.div(i, n // 2)
         return i if g < phases - 1 else (1 - far) * i + far * (n // 2 + lax.rem(i + n // 4, n // 2))
 
-    def width_of(g):
-        return vp if g < phases - 1 else vp - LANES
-
     def load(g, k, width):
         col, _ = window(k)
         return pltpu.make_async_copy(q_ref.at[g * ROWS:(g + 1) * ROWS, pl.ds(col, width)], sbuf.at[g, k, :, pl.ds(0, width)], ld_sem.at[g, k])
 
-    def q_copy(g, r, s):
+    def q_copy(stage, r, s):
         a, b = peer(r)
+        k = a * 4 + b
+        if stage == 0:
+            src, dst = sbuf.at[0:phases - 1, k, :, pl.ds(0, vp)], qbuf.at[0:phases - 1, s]
+        else:
+            src, dst = sbuf.at[phases - 1, k, :, pl.ds(0, vp - LANES)], qbuf.at[phases - 1, s, :, pl.ds(0, vp - LANES)]
         return pltpu.make_async_remote_copy(
-            src_ref=sbuf.at[g, a * 4 + b, :, pl.ds(0, width_of(g))], dst_ref=qbuf.at[g, s, :, pl.ds(0, width_of(g))],
-            send_sem=qs_sem.at[g, r], recv_sem=qr_sem.at[g, s],
+            src_ref=src, dst_ref=dst, send_sem=qs_sem.at[stage, r], recv_sem=qr_sem.at[stage, s],
             device_id={"tpa": a, "tpb": b}, device_id_type=MESH)
 
     def tile_of(j):
@@ -110,40 +109,38 @@
             this = following
         sbuf[g, k, :, tile_of(tiles - 1)] = ending
 
-    def ready(g, i):
-        if g < phases - 1:
+    def ready(stage, i):
+        r = nth(stage, i)
+        a, b = peer(r)
+        k = a * 4 + b
+        if stage == 0:
             @pl.when(i + AHEAD < n)
             def _():
-                start_load(g, i + AHEAD)
-        r = nth(g, i)
-        a, b = peer(r)
-        k = a * 4 + b
-        if g == 0:
-            sized(k, lambda width: load(0, k, width).wait())
-            sized(k, lambda width: load(phases - 1, k, width).wait())
-        elif g < phases - 1:
-            sized(k, lambda width: load(g, k, width).wait())
-        prepare(g, k)
-
-        @pl.when(r == 0)
-        def _():
-            for j in range(tiles):
-                qbuf[g, me, :, tile_of(j)] = sbuf[g, me, :, tile_of(j)]
-
-    def first(g):
-        lax.fori_loop(0, 2, lambda i, c: (ready(g, i), c)[1], 0)
-
-    def send_phase(g):
+                start_load(i + AHEAD)
+            for g in range(phases):
+                sized(k, lambda width, g=g: load(g, k, width).wait())
+        for g in range(phases - 1) if stage == 0 else (phases - 1,):
+            prepare(g, k)
+
+            @pl.when(r == 0)
+            def _(g=g):
+                for j in range(tiles):
+                    qbuf[g, me, :, tile_of(j)] = sbuf[g, me, :, tile_of(j)]
+
+    def first(stage):
+        lax.fori_loop(0, 2, lambda i, c: (ready(stage, i), c)[1], 0)
+
+    def send_stage(stage):
         def one(i, c):
-            r = nth(g, i)
+            r = nth(stage, i)
 
             @pl.when(r > 0)
             def _():
-                q_copy(g, r, me).start()
+                q_copy(stage, r, me).start()
 
             @pl.when(i + 2 < n)
             def _():
-                ready(g, i + 2)
+                ready(stage, i + 2)
             return c
         lax.fori_loop(0, n, one, 0)
 
@@ -164,28 +161,22 @@
         a, b = peer(r)
         pl.semaphore_signal(barrier, inc=1, device_id={"tpa": a, "tpb": b}, device_id_type=MESH)
 
-    def start_load(g, i):
-        a, b = peer(nth(g, i))
+    def start_load(i):
+        a, b = peer(nth(0, i))
         k = a * 4 + b
-        for h in (0, phases - 1) if g == 0 else (g,):
-            sized(k, lambda width, h=h: load(h, k, width).start())
+        for g in range(phases):
+            sized(k, lambda width, g=g: load(g, k, width).start())
 
     for i in range(AHEAD):
-        start_load(0, i)
+        start_load(i)
     x_copy.start()
     first(0)
     pl.semaphore_wait(barrier, n - 1)
 
-    send_phase(0)
-    for g in range(1, phases - 1):
-        for i in range(AHEAD):
-            start_load(g, i)
+    send_stage(0)
     hid_copy.start()
     for c in range(W_BUFS):
         w_copy(c, c).start()
-    for g in range(1, phases - 1):
-        first(g)
-        send_phase(g)
 
     hid_copy.wait()
     row = lax.broadcasted_iota(jnp.int32, (rows_all, rows_all), 0)
@@ -297,8 +288,8 @@
     stat_chip[chip, 0] = jnp.where(mine, top[0:half], top[half:])
     stat_chip[chip, 1] = jnp.where(mine, total[0:half], total[half:])
     chip_send(0, stat_chip)
-    first(phases - 1)
-    send_phase(phases - 1)
+    first(1)
+    send_stage(1)
 
     chip_arrivals(0, stat_chip)
     top, total = combine([(stat_chip[c, 0], stat_chip[c, 1]) for c in range(chips)])
@@ -371,9 +362,10 @@
             a, b = peer(r)
             s = a * 4 + b
 
-            @pl.when(r > 0)
-            def _():
-                q_copy(g, r, s).wait_recv()
+            if g in (0, phases - 1):
+                @pl.when(r > 0)
+                def _():
+                    q_copy(min(g, 1), r, s).wait_recv()
             excess(g, s)
             return c
         lax.fori_loop(0, n, one, 0)
@@ -389,8 +381,8 @@
         z_copy(r, me).start()
 
     def drain(r, c):
-        for g in range(phases):
-            q_copy(g, r, me).wait_send()
+        for stage in range(2):
+            q_copy(stage, r, me).wait_send()
         z_copy(r, me).wait_send()
         return c
 
@@ -542,8 +534,8 @@
                 pltpu.SemaphoreType.DMA((2,)),
                 pltpu.SemaphoreType.DMA((W_BUFS,)),
                 pltpu.SemaphoreType.DMA((phases, n)),
-                pltpu.SemaphoreType.DMA((phases, n)),
-                pltpu.SemaphoreType.DMA((phases, n)),
+                pltpu.SemaphoreType.DMA((2, n)),
+                pltpu.SemaphoreType.DMA((2, n)),
                 pltpu.SemaphoreType.DMA((4,)),
                 pltpu.SemaphoreType.DMA((4,)),
                 pltpu.SemaphoreType.DMA((2, n // 2)),

time: 287 us -> 290 us (1.010)
  Pallas kernels: 286 us -> 289 us
where the time goes in v10:
time: 290 us
  Pallas kernels  289 us (100%)
    pallas_call x1, Pallas kernels, local_step(): pl.pallas_call(functools.partial(exchange_kernel, n, phases, vl), name='e...  284 us

profile of v10, /device:TPU:0, one launch (start us, length us, event | category | flops | bytes accessed | tf_op | source)
XLA Modules:
  0.0 289.7 jit_solution(6569999481287425386)
XLA Ops:
  0.6 284.0 %exchange.1 = (f32[400,8016]{1,0:T(8,128)S(1)}, f32[3,3,128]{2,1,0:T(4,128)S(1)}) custom-call(bf16[400,3072]{1,0:T(8,128)(2,1)} %bitcast.8, bf16[8016,3072]{1,0:T(8,128)(2,1)} %bitcast.6, f32[24,128256]{1,0:T(8,128)} %bitcast.7, s32[16,24]{1,0:T(8,128)} %x_ref.1), custom_call_target="tpu_custom_call" | custom-call | tf_op jit(solution)/shard_map/exchange/pallas_call | solution.py:510
  284.6 5.1 %finish.1 = (f32[16,24,8016]{2,1,0:T(8,128)}, f32[16,8016]{1,0:T(8,128)}, f32[16,24]{1,0:T(8,128)}, f32[1,16]{1,0:T(1,128)}) custom-call(f32[3,3,128]{2,1,0:T(4,128)S(1)} %get-tuple-element.10.tot_ref, f32[400,8016]{1,0:T(8,128)S(1)} %get-tuple-element.11.z_ref), custom_call_target="tpu_custom_call" | custom-call | tf_op jit(solution)/shard_map/finish/pallas_call | solution.py:548

commit v11 on v8

--- a/solution.py
+++ b/solution.py
@@ -14,6 +14,7 @@
 ROWS = 8
 W_ROWS = 256
 W_BUFS = 4
+PIECES = 2
 AHEAD = 4
 SCALE = 2.0 ** 64
 
@@ -58,13 +59,11 @@
     inner = lax.rem(lax.div(my_a + 1, 2), 2)
 
     def nth(g, i):
-        if g < phases - 1:
-            return inner * lax.rem((n // 2 + 1) * (i + core) + n // 2, n) + (1 - inner) * i
-        j = lax.div(i, 2)
-        is_far = lax.rem(i + core + 1, 2)
-        by_turns = is_far * jnp.where(j < n // 4, 3 * n // 4 - 1 - j, n + n // 4 - 1 - j) + (1 - is_far) * j
-        in_turn = jnp.where(i < n // 2, i, n + n // 2 - 1 - i)
-        return inner * by_turns + (1 - inner) * in_turn
+        r = inner * lax.rem((n // 2 + 1) * (i + core) + n // 2, n) + (1 - inner) * i
+        if g == phases - 1:
+            far = lax.div(r, n // 2)
+            r = (1 - far) * r + far * (n // 2 + lax.rem(r + (1 - inner) * (n // 4), n // 2))
+        return r
 
     def arrival_order(g, i):
         far = lax.div(i, n // 2)
@@ -82,6 +81,15 @@
         return pltpu.make_async_remote_copy(
             src_ref=sbuf.at[g, a * 4 + b, :, pl.ds(0, width_of(g))], dst_ref=qbuf.at[g, s, :, pl.ds(0, width_of(g))],
             send_sem=qs_sem.at[g, r], recv_sem=qr_sem.at[g, s],
+            device_id={"tpa": a, "tpb": b}, device_id_type=MESH)
+
+    def q_piece(g, r, h):
+        a, b = peer(r)
+        cut = [tiles * i // PIECES * LANES for i in range(PIECES)] + [width_of(g)]
+        at = pl.ds(cut[h], cut[h + 1] - cut[h])
+        return pltpu.make_async_remote_copy(
+            src_ref=sbuf.at[g, a * 4 + b, :, at], dst_ref=qbuf.at[g, me, :, at],
+            send_sem=qs_sem.at[g, r], recv_sem=qr_sem.at[g, me],
             device_id={"tpa": a, "tpb": b}, device_id_type=MESH)
 
     def tile_of(j):
@@ -134,18 +142,20 @@
         lax.fori_loop(0, 2, lambda i, c: (ready(g, i), c)[1], 0)
 
     def send_phase(g):
-        def one(i, c):
-            r = nth(g, i)
-
-            @pl.when(r > 0)
-            def _():
-                q_copy(g, r, me).start()
-
-            @pl.when(i + 2 < n)
-            def _():
-                ready(g, i + 2)
-            return c
-        lax.fori_loop(0, n, one, 0)
+        for h in range(PIECES):
+            def one(i, c, h=h):
+                r = nth(g, i)
+
+                @pl.when(r > 0)
+                def _():
+                    q_piece(g, r, h).start()
+
+                if h == 0:
+                    @pl.when(i + 2 < n)
+                    def _():
+                        ready(g, i + 2)
+                return c
+            lax.fori_loop(0, n, one, 0)
 
     def w_copy(c, slot):
         return pltpu.make_async_copy(w_ref.at[pl.ds(pl.multiple_of(c * W_ROWS, W_ROWS), W_ROWS), :], wbuf.at[slot], w_sem.at[slot])

time: 287 us -> 286 us (level)
  no operation moved by 1% of the time
where the time goes in v11:
time: 286 us; the launch traced here: 285 us
  Pallas kernels  285 us (100%)
    pallas_call x1, Pallas kernels, local_step(): pl.pallas_call(functools.partial(exchange_kernel, n, phases, vl), name='e...  280 us

profile of v11, /device:TPU:0, one launch (start us, length us, event | category | flops | bytes accessed | tf_op | source)
XLA Modules:
  0.0 285.3 jit_solution(743167077752197845)
XLA Ops:
  0.6 279.5 %exchange.1 = (f32[400,8016]{1,0:T(8,128)S(1)}, f32[3,3,128]{2,1,0:T(4,128)S(1)}) custom-call(bf16[400,3072]{1,0:T(8,128)(2,1)} %bitcast.8, bf16[8016,3072]{1,0:T(8,128)(2,1)} %bitcast.6, f32[24,128256]{1,0:T(8,128)} %bitcast.7, s32[16,24]{1,0:T(8,128)} %x_ref.1), custom_call_target="tpu_custom_call" | custom-call | tf_op jit(solution)/shard_map/exchange/pallas_call | solution.py:528
  280.2 5.1 %finish.1 = (f32[16,24,8016]{2,1,0:T(8,128)}, f32[16,8016]{1,0:T(8,128)}, f32[16,24]{1,0:T(8,128)}, f32[1,16]{1,0:T(1,128)}) custom-call(f32[3,3,128]{2,1,0:T(4,128)S(1)} %get-tuple-element.10.tot_ref, f32[400,8016]{1,0:T(8,128)S(1)} %get-tuple-element.11.z_ref), custom_call_target="tpu_custom_call" | custom-call | tf_op jit(solution)/shard_map/finish/pallas_call | solution.py:566

commit v12 on v11

--- a/solution.py
+++ b/solution.py
@@ -14,7 +14,7 @@
 ROWS = 8
 W_ROWS = 256
 W_BUFS = 4
-PIECES = 2
+PIECES = 4
 AHEAD = 4
 SCALE = 2.0 ** 64
 

time: 286 us -> 284 us (level)
  no operation moved by 1% of the time
where the time goes in v12:
time: 284 us
  Pallas kernels  283 us (100%)
    pallas_call x1, Pallas kernels, local_step(): pl.pallas_call(functools.partial(exchange_kernel, n, phases, vl), name='e...  278 us

profile of v12, /device:TPU:0, one launch (start us, length us, event | category | flops | bytes accessed | tf_op | source)
XLA Modules:
  0.0 284.1 jit_solution(12011516873223089328)
XLA Ops:
  0.6 278.4 %exchange.1 = (f32[400,8016]{1,0:T(8,128)S(1)}, f32[3,3,128]{2,1,0:T(4,128)S(1)}) custom-call(bf16[400,3072]{1,0:T(8,128)(2,1)} %bitcast.8, bf16[8016,3072]{1,0:T(8,128)(2,1)} %bitcast.6, f32[24,128256]{1,0:T(8,128)} %bitcast.7, s32[16,24]{1,0:T(8,128)} %x_ref.1), custom_call_target="tpu_custom_call" | custom-call | tf_op jit(solution)/shard_map/exchange/pallas_call | solution.py:528
  279.0 5.1 %finish.1 = (f32[16,24,8016]{2,1,0:T(8,128)}, f32[16,8016]{1,0:T(8,128)}, f32[16,24]{1,0:T(8,128)}, f32[1,16]{1,0:T(1,128)}) custom-call(f32[3,3,128]{2,1,0:T(4,128)S(1)} %get-tuple-element.10.tot_ref, f32[400,8016]{1,0:T(8,128)S(1)} %get-tuple-element.11.z_ref), custom_call_target="tpu_custom_call" | custom-call | tf_op jit(solution)/shard_map/finish/pallas_call | solution.py:566

commit v13 on v12

--- a/solution.py
+++ b/solution.py
@@ -14,7 +14,7 @@
 ROWS = 8
 W_ROWS = 256
 W_BUFS = 4
-PIECES = 4
+PIECES = 8
 AHEAD = 4
 SCALE = 2.0 ** 64
 

time: 284 us -> 285 us (level)
  no operation moved by 1% of the time
where the time goes in v13:
time: 285 us; the launch traced here: 284 us
  Pallas kernels  284 us (100%)
    pallas_call x1, Pallas kernels, local_step(): pl.pallas_call(functools.partial(exchange_kernel, n, phases, vl), name='e...  279 us

profile of v13, /device:TPU:0, one launch (start us, length us, event | category | flops | bytes accessed | tf_op | source)
XLA Modules:
  0.0 284.3 jit_solution(2865541200387827287)
XLA Ops:
  0.6 278.6 %exchange.1 = (f32[400,8016]{1,0:T(8,128)S(1)}, f32[3,3,128]{2,1,0:T(4,128)S(1)}) custom-call(bf16[400,3072]{1,0:T(8,128)(2,1)} %bitcast.8, bf16[8016,3072]{1,0:T(8,128)(2,1)} %bitcast.6, f32[24,128256]{1,0:T(8,128)} %bitcast.7, s32[16,24]{1,0:T(8,128)} %x_ref.1), custom_call_target="tpu_custom_call" | custom-call | tf_op jit(solution)/shard_map/exchange/pallas_call | solution.py:528
  279.2 5.1 %finish.1 = (f32[16,24,8016]{2,1,0:T(8,128)}, f32[16,8016]{1,0:T(8,128)}, f32[16,24]{1,0:T(8,128)}, f32[1,16]{1,0:T(1,128)}) custom-call(f32[3,3,128]{2,1,0:T(4,128)S(1)} %get-tuple-element.10.tot_ref, f32[400,8016]{1,0:T(8,128)S(1)} %get-tuple-element.11.z_ref), custom_call_target="tpu_custom_call" | custom-call | tf_op jit(solution)/shard_map/finish/pallas_call | solution.py:566

commit v14 on v12

--- a/solution.py
+++ b/solution.py
@@ -59,7 +59,7 @@
     inner = lax.rem(lax.div(my_a + 1, 2), 2)
 
     def nth(g, i):
-        r = inner * lax.rem((n // 2 + 1) * (i + core) + n // 2, n) + (1 - inner) * i
+        r = lax.rem((n // 2 + 1) * (i + core) + n // 2, n)
         if g == phases - 1:
             far = lax.div(r, n // 2)
             r = (1 - far) * r + far * (n // 2 + lax.rem(r + (1 - inner) * (n // 4), n // 2))

time: 284 us -> 287 us (1.011)
  Pallas kernels: 283 us -> 286 us
where the time goes in v14:
time: 287 us
  Pallas kernels  286 us (100%)
    pallas_call x1, Pallas kernels, local_step(): pl.pallas_call(functools.partial(exchange_kernel, n, phases, vl), name='e...  281 us

profile of v14, /device:TPU:0, one launch (start us, length us, event | category | flops | bytes accessed | tf_op | source)
XLA Modules:
  0.0 286.9 jit_solution(12047804979389523448)
XLA Ops:
  0.6 281.2 %exchange.1 = (f32[400,8016]{1,0:T(8,128)S(1)}, f32[3,3,128]{2,1,0:T(4,128)S(1)}) custom-call(bf16[400,3072]{1,0:T(8,128)(2,1)} %bitcast.8, bf16[8016,3072]{1,0:T(8,128)(2,1)} %bitcast.6, f32[24,128256]{1,0:T(8,128)} %bitcast.7, s32[16,24]{1,0:T(8,128)} %x_ref.1), custom_call_target="tpu_custom_call" | custom-call | tf_op jit(solution)/shard_map/exchange/pallas_call | solution.py:528
  281.9 5.1 %finish.1 = (f32[16,24,8016]{2,1,0:T(8,128)}, f32[16,8016]{1,0:T(8,128)}, f32[16,24]{1,0:T(8,128)}, f32[1,16]{1,0:T(1,128)}) custom-call(f32[3,3,128]{2,1,0:T(4,128)S(1)} %get-tuple-element.10.tot_ref, f32[400,8016]{1,0:T(8,128)S(1)} %get-tuple-element.11.z_ref), custom_call_target="tpu_custom_call" | custom-call | tf_op jit(solution)/shard_map/finish/pallas_call | solution.py:566
